TPU v7x, 256 devices: a whole 4x4x8 slice. The times are simulated.
256 devices in a mesh: rows: 32 (over z, y), chan: 8 (over x, core).
Axes of the slice: x: 4, y: 4, z: 8, core: 2. Of those that a mesh axis runs over, the one named last changes fastest.
Arguments:
- tokens: float32 [64, 768, 512], P('rows', 'chan'), may hold values from -6 to 6
- spectral: float32 [2, 64, 768, 128], P(None, None, 'chan'), may hold values from -6 to 6
- gain_in: float32 [2, 768], P(None, 'chan'), may hold values from 0.25 to 1.75
- gain_mid: float32 [2, 768], P(None, 'chan'), may hold values from 0.25 to 1.75
- expand: bfloat16 [2, 768, 3072], P(None, 'rows', 'chan'), may hold values from -0.21875 to 0.21875
- expand_bias: bfloat16 [2, 3072], P(None, 'chan'), may hold values from -3 to 3
- shrink: bfloat16 [2, 3072, 768], P(None, 'chan', 'rows'), may hold values from -0.21875 to 0.21875
Outputs:
- result: float32 [64, 768, 512], P('rows', 'chan')
All inputs are finite; a program needn't handle non-finite values.
Results may differ from a plain program's by a relative error of at most 0.017.
Values may be sent and summed in bfloat16 or wider, within the bound.
A program may use at most 64 MiB of HBM per device.

v0:
```python
import math

import jax
import jax.numpy as jnp
from jax import lax
from jax.sharding import Mesh
from jax.sharding import PartitionSpec as P

GRID = 64
CHAN = ("chan_0", "chan_1")


def from_everyone(value, axis):
    copies = jnp.broadcast_to(value, (lax.axis_size(axis), *value.shape))
    return lax.all_to_all(copies, axis, split_axis=0, concat_axis=0, tiled=True)


def taken_together(value, axis):
    return from_everyone(value, axis).sum(axis=0)


def in_one(arrays, axis):
    flat, at, finished = (jnp.concatenate([a.reshape(-1) for a in arrays]), 0, [])
    running = taken_together(flat, axis)
    for a in arrays:
        finished.append(running[at : at + a.size].reshape(a.shape))
        at += a.size
    return tuple(finished)


def sent_together(arrays, axis, split_dim, concat_dim, along):
    widths = [a.shape[along] for a in arrays]
    both = jnp.concatenate(arrays, axis=along)
    out = lax.all_to_all(both, axis, split_axis=split_dim, concat_axis=concat_dim, tiled=True)
    return tuple(jnp.split(out, [sum(widths[:k]) for k in range(1, len(widths))], axis=along))


def cut_rows(length, count):
    unit = 8 if length >= 8 * count else 1
    return [length // unit * k // count * unit for k in range(1, count)]


def stacked_from(value, axes, sequence):
    tiles = value[None]
    for k in sequence:
        tiles = lax.all_gather(tiles, axes[k], axis=0, tiled=True)
    held = [lax.axis_size(axes[k]) for k in reversed(sequence)]
    tiles = tiles.reshape(*held, *value.shape)
    turned = sorted(range(len(sequence)), key=lambda place: sequence[len(sequence) - 1 - place])
    return tiles.transpose(*turned, *range(len(sequence), tiles.ndim)).reshape(-1, *value.shape)


def in_order(tiles, dim):
    dims = list(tiles.shape[1:])
    dims[dim] *= tiles.shape[0]
    return jnp.moveaxis(tiles, 0, dim).reshape(dims)


def spread_gather(value, axes, dim):
    widest = max(range(max(1, value.ndim - 1)), key=lambda d: value.shape[d])
    count, finished = (len(axes), [])
    for leading, share in enumerate(
        jnp.split(value, cut_rows(value.shape[widest], count), axis=widest)
    ):
        if share.size:
            sequence = [(leading - k) % count for k in range(count)]
            finished.append(stacked_from(share, axes, sequence))
    return in_order(jnp.concatenate(finished, axis=widest + 1), dim)


def gather_directly(value, axis, dim):
    return in_order(from_everyone(value, axis), dim)


def in_blocks(value, dim, peers):
    before, after = (value.shape[:dim], value.shape[dim + 1 :])
    return jnp.moveaxis(value.reshape(*before, peers, -1, *after), dim, 0)


def summed_on_arrival(value, axis, dim):
    tiles = in_blocks(value, dim, lax.axis_size(axis))
    arrived = lax.all_to_all(tiles, axis, split_axis=0, concat_axis=0, tiled=True)
    return arrived.astype(jnp.float32).sum(axis=0)


def tables(count):
    index = jnp.arange(count, dtype=jnp.int32)
    product = index[:, None] * index[None, :] % count
    angle = product.astype(jnp.float32) * (2.0 * math.pi / count)
    return (jnp.cos(angle), jnp.sin(angle))


def finish_norm(values, sums, squares, total, gain):
    mean = sums / total
    var = squares / total - mean * mean
    return (values - mean[:, None, :]) * lax.rsqrt(var + 1e-06)[:, None, :] * gain[None, :, None]


def reflect(values):
    return jnp.roll(jnp.flip(values, -1), 1, -1)


def row_transform(a_re, a_im, cosine, sine, highest):
    b_re = jnp.einsum("hcbk,hj->cbkj", a_re, cosine, precision=highest) + jnp.einsum(
        "hcbk,hj->cbkj", a_im, sine, precision=highest
    )
    b_im = jnp.einsum("hcbk,hj->cbkj", a_im, cosine, precision=highest) - jnp.einsum(
        "hcbk,hj->cbkj", a_re, sine, precision=highest
    )
    return (b_re, b_im)


def row_inverse(c_re, c_im, cosine, sine, highest):
    d_re = jnp.einsum("cbkj,jh->hcbk", c_re, cosine, precision=highest) - jnp.einsum(
        "cbkj,jh->hcbk", c_im, sine, precision=highest
    )
    d_im = jnp.einsum("cbkj,jh->hcbk", c_im, cosine, precision=highest) + jnp.einsum(
        "cbkj,jh->hcbk", c_re, sine, precision=highest
    )
    return (d_re, d_im)


def per_device(tokens, spectral, gain_in, gain_mid, expand, expand_bias, shrink):
    highest = lax.Precision.HIGHEST
    local_rows, local_chan, merged = tokens.shape
    channels = local_chan * lax.axis_size(CHAN)
    images = merged // GRID
    cosine, sine = tables(GRID)
    half = GRID // 2
    parity = jnp.where(jnp.arange(GRID, dtype=jnp.int32) % 2 == 0, 1.0, -1.0).astype(jnp.float32)
    state = tokens
    for layer in range(expand.shape[0]):
        sums = in_one((jnp.sum(state, axis=1), jnp.sum(state * state, axis=1)), CHAN)
        normed = finish_norm(state, sums[0], sums[1], channels, gain_in[layer]).reshape(
            local_rows, local_chan, images, GRID
        )
        spec_layer = spectral[layer]
        cos_half = cosine[:, :half]
        sin_half = (-sine[:, :half]).at[:, 0].set(parity)
        a_re = jnp.einsum("hcbw,wk->hcbk", normed, cos_half, precision=highest)
        a_im = jnp.einsum("hcbw,wk->hcbk", normed, sin_half, precision=highest)
        a_re, a_im = tuple(
            (
                part.astype(jnp.float32)
                for part in sent_together(
                    (a_re.astype(jnp.bfloat16), a_im.astype(jnp.bfloat16)), "rows", 3, 0, 1
                )
            )
        )
        b_re, b_im = row_transform(a_re, a_im, cosine, sine, highest)
        owned = a_re.shape[3]
        column = lax.axis_index("rows") * owned + jnp.arange(owned, dtype=jnp.int32)
        mine = jnp.take(spec_layer, column, axis=0)
        mirror = jnp.take(spec_layer, (GRID - column) % GRID, axis=0)
        g_re = (mine[:, :, :GRID] + reflect(mirror[:, :, :GRID])).transpose(1, 0, 2)[:, None]
        g_im = (mine[:, :, GRID:] - reflect(mirror[:, :, GRID:])).transpose(1, 0, 2)[:, None]
        gen_re = b_re * g_re - b_im * g_im
        gen_im = b_re * g_im + b_im * g_re
        first = spec_layer[0]
        middle_col = spec_layer[half]
        low_re = 0.5 * (first[:, :GRID] + reflect(first[:, :GRID]))
        low_im = 0.5 * (first[:, GRID:] - reflect(first[:, GRID:]))
        top_re = 0.5 * (middle_col[:, :GRID] + reflect(middle_col[:, :GRID]))
        top_im = 0.5 * (middle_col[:, GRID:] - reflect(middle_col[:, GRID:]))
        plus_re = (0.5 * (low_re + top_re))[:, None, None, :]
        plus_im = (0.5 * (low_im + top_im))[:, None, None, :]
        minus_re = (0.5 * (low_re - top_re))[:, None, None, :]
        minus_im = (0.5 * (low_im - top_im))[:, None, None, :]
        back_re = reflect(b_re)
        back_im = -reflect(b_im)
        zero_re = b_re * plus_re - b_im * plus_im + back_re * minus_re - back_im * minus_im
        zero_im = b_re * plus_im + b_im * plus_re + back_re * minus_im + back_im * minus_re
        is_zero = (column == 0)[None, None, :, None]
        c_re = jnp.where(is_zero, zero_re, gen_re)
        c_im = jnp.where(is_zero, zero_im, gen_im)
        d_re, d_im = row_inverse(c_re, c_im, cosine, sine, highest)
        d_re, d_im = tuple(
            (
                part.astype(jnp.float32)
                for part in sent_together(
                    (d_re.astype(jnp.bfloat16), d_im.astype(jnp.bfloat16)), "rows", 0, 3, 1
                )
            )
        )
        last_sin = sine[:half, :].at[0, :].set(-parity)
        mixed = (
            jnp.einsum("hcbk,kw->hcbw", d_re, cosine[:half, :], precision=highest)
            - jnp.einsum("hcbk,kw->hcbw", d_im, last_sin, precision=highest)
        ) * (1.0 / (GRID * GRID))
        mixed = mixed.reshape(local_rows, local_chan, merged)
        middle = in_one((jnp.sum(mixed, axis=1), jnp.sum(mixed * mixed, axis=1)), CHAN)
        normed2 = finish_norm(mixed, middle[0], middle[1], channels, gain_mid[layer]).astype(
            jnp.bfloat16
        )
        flat = normed2.transpose(0, 2, 1).reshape(-1, local_chan)
        whole = spread_gather(flat, CHAN, 1)
        pre = jnp.dot(
            whole, gather_directly(expand[layer], "rows", 0), preferred_element_type=jnp.float32
        )
        hidden = jax.nn.gelu(pre + expand_bias[layer].astype(jnp.float32), approximate=True).astype(
            jnp.bfloat16
        )
        terms = jnp.dot(
            hidden, gather_directly(shrink[layer], "rows", 1), preferred_element_type=jnp.float32
        )
        branch = summed_on_arrival(terms.astype(jnp.bfloat16), CHAN, 1).astype(jnp.bfloat16)
        update = (
            branch.astype(jnp.float32).reshape(local_rows, merged, local_chan).transpose(0, 2, 1)
        )
        state = state + update
    return state


def solution(mesh):
    torus = Mesh(mesh.devices.reshape(mesh.shape["rows"], 4, 2), ("rows", "chan_0", "chan_1"))
    placed = (
        P("rows", CHAN, None),
        P(None, None, CHAN, None),
        P(None, CHAN),
        P(None, CHAN),
        P(None, "rows", CHAN),
        P(None, CHAN),
        P(None, CHAN, "rows"),
    )
    return jax.shard_map(
        per_device, mesh=torus, in_specs=placed, out_specs=P("rows", CHAN, None), check_vma=False
    )
```

profile of v0, /device:TPU:1, one launch (start us, length us, event | category | flops | bytes accessed | tf_op | source)
XLA Modules:
  0.0 321.1 jit_solution(17089204497144788136)
XLA Ops:
  1.8 6.5 %all-to-all-start = ((f32[8,1,2048]{2,1,0:T(1,128)}), f32[8,1,2048]{2,1,0:T(1,128)S(1)}, u32[]{:S(2)}, u32[]{:S(2)}) async-start(f32[8,1,2048]{2,1,0:T(1,128)} %broadcast_in_dim.92), calls=%async_computation | async-start | bytes 131072 | tf_op jit(solution)/shard_map/all_to_all | solution.py:15
  17.7 10.5 %all-to-all-start.1 = ((bf16[2,192,8,32]{1,2,0,3:T(8,128)(2,1)}), bf16[2,192,8,32]{1,2,0,3:T(8,128)(2,1)S(1)}, u32[]{:S(2)}, u32[]{:S(2)}) async-start(bf16[2,192,8,32]{1,2,0,3:T(8,128)(2,1)} %copy.230), calls=%async_computation.1 | async-start | bytes 524288 | tf_op jit(solution)/shard_map/all_to_all | solution.py:34
  29.0 11.2 %all-to-all-done.1 = bf16[2,192,8,32]{1,2,0,3:T(8,128)(2,1)S(1)} async-done(((bf16[2,192,8,32]{1,2,0,3:T(8,128)(2,1)}), bf16[2,192,8,32]{1,2,0,3:T(8,128)(2,1)S(1)}, u32[]{:S(2)}, u32[]{:S(2)}) %all-to-all-start.1) | async-done | bytes 196640 | tf_op jit(solution)/shard_map/all_to_all | solution.py:34
  50.1 10.2 %all-to-all-done.2 = bf16[64,192,8,1]{1,2,3,0:T(8,128)(2,1)S(1)} async-done(((bf16[64,192,8,1]{1,2,3,0:T(8,128)(2,1)}), bf16[64,192,8,1]{1,2,3,0:T(8,128)(2,1)S(1)}, u32[]{:S(2)}, u32[]{:S(2)}) %all-to-all-start.2) | async-done | bytes 196640 | tf_op jit(solution)/shard_map/all_to_all | solution.py:34
  62.3 7.9 %all-to-all-start.3 = ((f32[8,1,2048]{2,1,0:T(1,128)}), f32[8,1,2048]{2,1,0:T(1,128)S(1)}, u32[]{:S(2)}, u32[]{:S(2)}) async-start(f32[8,1,2048]{2,1,0:T(1,128)} %broadcast_in_dim.97), calls=%async_computation.3 | async-start | bytes 131072 | tf_op jit(solution)/shard_map/all_to_all | solution.py:15
  70.2 4.8 %all-to-all-done.3 = f32[8,1,2048]{2,1,0:T(1,128)S(1)} async-done(((f32[8,1,2048]{2,1,0:T(1,128)}), f32[8,1,2048]{2,1,0:T(1,128)S(1)}, u32[]{:S(2)}, u32[]{:S(2)}) %all-to-all-start.3) | async-done | bytes 65568 | tf_op jit(solution)/shard_map/all_to_all | solution.py:15
  80.2 17.2 %all-to-all-done.4 = bf16[32,24,384]{2,1,0:T(8,128)(2,1)S(1)} async-done(((bf16[32,24,384]{2,1,0:T(8,128)(2,1)}), bf16[32,24,384]{2,1,0:T(8,128)(2,1)S(1)}, u32[]{:S(2)}, u32[]{:S(2)}) %all-to-all-start.4) | async-done | bytes 589856 | tf_op jit(solution)/shard_map/all_to_all | solution.py:15
  98.3 5.2 %all-to-all-start.5 = ((bf16[32,384,24]{1,2,0:T(8,128)(2,1)}), bf16[32,384,24]{1,2,0:T(8,128)(2,1)S(1)}, u32[]{:S(2)}, u32[]{:S(2)}) async-start(bf16[32,384,24]{1,2,0:T(8,128)(2,1)} %broadcast_in_dim.99), calls=%async_computation.5 | async-start | bytes 1179648 | tf_op jit(solution)/shard_map/all_to_all | solution.py:15
  103.6 10.5 %all_gather.24 = bf16[4,512,96]{1,2,0:T(8,128)(2,1)S(1)} all-gather(bf16[1,512,96]{1,2,0:T(8,128)(2,1)S(1)} %get-tuple-element.96), channel_id=1, replica_groups=mesh['rows'=32,'chan_0'=4,'chan_1'=2] {'chan_0'}, dimensions={0}, use_global_device_ids=true | all-gather | bytes 491520 | tf_op jit(solution)/shard_map/all_gather | solution.py:46
  114.2 6.0 %all_gather.25 = bf16[8,512,96]{1,2,0:T(8,128)(2,1)S(1)} all-gather(bf16[4,512,96]{1,2,0:T(8,128)(2,1)S(1)} %all_gather.24), channel_id=1, replica_groups=mesh['rows'=32,'chan_0'=4,'chan_1'=2] {'chan_1'}, dimensions={0}, use_global_device_ids=true | all-gather | bytes 1179648 | tf_op jit(solution)/shard_map/all_gather | solution.py:46
  122.2 11.1 %all_gather.27 = bf16[8,512,96]{1,2,0:T(8,128)(2,1)S(1)} all-gather(bf16[2,512,96]{1,2,0:T(8,128)(2,1)S(1)} %all_gather.26), channel_id=1, replica_groups=mesh['rows'=32,'chan_0'=4,'chan_1'=2] {'chan_0'}, dimensions={0}, use_global_device_ids=true | all-gather | bytes 983040 | tf_op jit(solution)/shard_map/all_gather | solution.py:46
  136.7 7.0 %all-to-all-start.6 = ((bf16[8,1024,96]{1,2,0:T(8,128)(2,1)}), bf16[8,1024,96]{1,2,0:T(8,128)(2,1)S(1)}, u32[]{:S(2)}, u32[]{:S(2)}) async-start(bf16[8,1024,96]{1,2,0:T(8,128)(2,1)} %bitcast.279), calls=%async_computation.6 | async-start | bytes 3145728 | tf_op jit(solution)/shard_map/all_to_all | solution.py:82
  144.3 20.1 %all-to-all-done.6 = bf16[8,1024,96]{1,2,0:T(8,128)(2,1)S(1)} async-done(((bf16[8,1024,96]{1,2,0:T(8,128)(2,1)}), bf16[8,1024,96]{1,2,0:T(8,128)(2,1)S(1)}, u32[]{:S(2)}, u32[]{:S(2)}) %all-to-all-start.6) | async-done | bytes 1572896 | tf_op jit(solution)/shard_map/all_to_all | solution.py:82
  170.1 4.4 %all-to-all-done.7 = f32[8,1,2048]{2,1,0:T(1,128)S(1)} async-done(((f32[8,1,2048]{2,1,0:T(1,128)}), f32[8,1,2048]{2,1,0:T(1,128)S(1)}, u32[]{:S(2)}, u32[]{:S(2)}) %all-to-all-start.7) | async-done | bytes 65568 | tf_op jit(solution)/shard_map/all_to_all | solution.py:15
  176.9 9.4 %all-to-all-start.8 = ((bf16[2,192,8,32]{1,2,0,3:T(8,128)(2,1)}), bf16[2,192,8,32]{1,2,0,3:T(8,128)(2,1)S(1)}, u32[]{:S(2)}, u32[]{:S(2)}) async-start(bf16[2,192,8,32]{1,2,0,3:T(8,128)(2,1)} %copy.251), calls=%async_computation.8 | async-start | bytes 524288 | tf_op jit(solution)/shard_map/all_to_all | solution.py:34
  187.0 10.6 %all-to-all-done.8 = bf16[2,192,8,32]{1,2,0,3:T(8,128)(2,1)S(1)} async-done(((bf16[2,192,8,32]{1,2,0,3:T(8,128)(2,1)}), bf16[2,192,8,32]{1,2,0,3:T(8,128)(2,1)S(1)}, u32[]{:S(2)}, u32[]{:S(2)}) %all-to-all-start.8) | async-done | bytes 196640 | tf_op jit(solution)/shard_map/all_to_all | solution.py:34
  202.2 14.9 %all_to_all.126 = bf16[64,192,8,1]{1,2,3,0:T(8,128)(2,1)S(1)} all-to-all(bf16[64,192,8,1]{1,2,3,0:T(8,128)(2,1)S(1)} %copy.262), channel_id=1, replica_groups=mesh['rows'=32,'chan_0'=4,'chan_1'=2] {'rows'}, dimensions={0} | all-to-all | bytes 393216 | tf_op jit(solution)/shard_map/all_to_all | solution.py:34
  218.5 11.0 %all_to_all.127 = f32[8,1,2048]{2,1,0:T(1,128)S(1)} all-to-all(f32[8,1,2048]{2,1,0:T(1,128)S(1)} %broadcast_in_dim.101), channel_id=1, replica_groups=mesh['rows'=32,'chan_0'=4,'chan_1'=2] {'chan_0','chan_1'}, dimensions={0} | all-to-all | bytes 131072 | tf_op jit(solution)/shard_map/all_to_all | solution.py:15
  234.5 17.3 %all-to-all-done.11 = bf16[32,24,384]{2,1,0:T(8,128)(2,1)S(1)} async-done(((bf16[32,24,384]{2,1,0:T(8,128)(2,1)}), bf16[32,24,384]{2,1,0:T(8,128)(2,1)S(1)}, u32[]{:S(2)}, u32[]{:S(2)}) %all-to-all-start.11) | async-done | bytes 589856 | tf_op jit(solution)/shard_map/all_to_all | solution.py:15
  252.7 5.3 %all-to-all-start.12 = ((bf16[32,384,24]{1,2,0:T(8,128)(2,1)}), bf16[32,384,24]{1,2,0:T(8,128)(2,1)}, u32[]{:S(2)}, u32[]{:S(2)}) async-start(bf16[32,384,24]{1,2,0:T(8,128)(2,1)} %broadcast_in_dim.103), calls=%async_computation.12 | async-start | bytes 1179648 | tf_op jit(solution)/shard_map/all_to_all | solution.py:15
  258.2 10.8 %all_gather.28 = bf16[4,512,96]{1,2,0:T(8,128)(2,1)S(1)} all-gather(bf16[1,512,96]{1,2,0:T(8,128)(2,1)S(1)} %get-tuple-element.94), channel_id=1, replica_groups=mesh['rows'=32,'chan_0'=4,'chan_1'=2] {'chan_0'}, dimensions={0}, use_global_device_ids=true | all-gather | bytes 491520 | tf_op jit(solution)/shard_map/all_gather | solution.py:46
  269.0 5.9 %all_gather.29 = bf16[8,512,96]{1,2,0:T(8,128)(2,1)S(1)} all-gather(bf16[4,512,96]{1,2,0:T(8,128)(2,1)S(1)} %all_gather.28), channel_id=1, replica_groups=mesh['rows'=32,'chan_0'=4,'chan_1'=2] {'chan_1'}, dimensions={0}, use_global_device_ids=true | all-gather | bytes 1179648 | tf_op jit(solution)/shard_map/all_gather | solution.py:46
  277.0 10.9 %all_gather.31 = bf16[8,512,96]{1,2,0:T(8,128)(2,1)S(1)} all-gather(bf16[2,512,96]{1,2,0:T(8,128)(2,1)S(1)} %all_gather.30), channel_id=1, replica_groups=mesh['rows'=32,'chan_0'=4,'chan_1'=2] {'chan_0'}, dimensions={0}, use_global_device_ids=true | all-gather | bytes 983040 | tf_op jit(solution)/shard_map/all_gather | solution.py:46
  292.3 27.6 %all_to_all.128 = bf16[8,1024,96]{1,2,0:T(8,128)(2,1)S(1)} all-to-all(bf16[8,1024,96]{1,2,0:T(8,128)(2,1)} %bitcast.282), channel_id=1, replica_groups=mesh['rows'=32,'chan_0'=4,'chan_1'=2] {'chan_0','chan_1'}, dimensions={0} | all-to-all | bytes 3145728 | tf_op jit(solution)/shard_map/all_to_all | solution.py:82
  (187 shorter events, 63.5 us)
Async XLA Ops:
  1.8 13.6 %all-to-all-start = ((f32[8,1,2048]{2,1,0:T(1,128)}), f32[8,1,2048]{2,1,0:T(1,128)S(1)}, u32[]{:S(2)}, u32[]{:S(2)}) async-start(f32[8,1,2048]{2,1,0:T(1,128)} %broadcast_in_dim.92), calls=%async_computation | async-start | bytes 131072 | tf_op jit(solution)/shard_map/all_to_all | solution.py:15
  8.2 3.6 %copy-start = (f32[2,96,512]{2,1,0:T(8,128)S(1)}, f32[2,96,512]{2,1,0:T(8,128)}, u32[]{:S(2)}) copy-start(f32[2,96,512]{2,1,0:T(8,128)} %param.17) | copy-start | bytes 1179652
  11.7 2.7 copy-start.4
  17.7 22.5 %all-to-all-start.1 = ((bf16[2,192,8,32]{1,2,0,3:T(8,128)(2,1)}), bf16[2,192,8,32]{1,2,0,3:T(8,128)(2,1)S(1)}, u32[]{:S(2)}, u32[]{:S(2)}) async-start(bf16[2,192,8,32]{1,2,0,3:T(8,128)(2,1)} %copy.230), calls=%async_computation.1 | async-start | bytes 524288 | tf_op jit(solution)/shard_map/all_to_all | solution.py:34
  45.5 24.7 %copy-start.1 = (bf16[2,24,384]{2,1,0:T(8,128)(2,1)S(1)}, bf16[2,24,384]{2,1,0:T(8,128)(2,1)}, u32[]{:S(2)}) copy-start(bf16[2,24,384]{2,1,0:T(8,128)(2,1)} %param.21) | copy-start | bytes 110596
  45.5 14.8 %all-to-all-start.2 = ((bf16[64,192,8,1]{1,2,3,0:T(8,128)(2,1)}), bf16[64,192,8,1]{1,2,3,0:T(8,128)(2,1)S(1)}, u32[]{:S(2)}, u32[]{:S(2)}) async-start(bf16[64,192,8,1]{1,2,3,0:T(8,128)(2,1)} %copy.241), calls=%async_computation.2 | async-start | bytes 524288 | tf_op jit(solution)/shard_map/all_to_all | solution.py:34
  60.7 19.1 %copy-start.3 = (bf16[2,384]{1,0:T(2,128)(2,1)S(1)}, bf16[2,384]{1,0:T(2,128)(2,1)}, u32[]{:S(2)}) copy-start(bf16[2,384]{1,0:T(2,128)(2,1)} %param.22) | copy-start | bytes 4612
  60.8 19.1 %copy-start.5 = (f32[2,96]{1,0:T(2,128)S(1)}, f32[2,96]{1,0:T(2,128)}, u32[]{:S(2)}) copy-start(f32[2,96]{1,0:T(2,128)} %param.20) | copy-start | bytes 2308
  60.8 19.1 %copy-start.2 = (bf16[2,384,24]{1,2,0:T(8,128)(2,1)S(1)}, bf16[2,384,24]{1,2,0:T(8,128)(2,1)}, u32[]{:S(2)}) copy-start(bf16[2,384,24]{1,2,0:T(8,128)(2,1)} %param.23) | copy-start | bytes 110596
  62.3 12.7 %all-to-all-start.3 = ((f32[8,1,2048]{2,1,0:T(1,128)}), f32[8,1,2048]{2,1,0:T(1,128)S(1)}, u32[]{:S(2)}, u32[]{:S(2)}) async-start(f32[8,1,2048]{2,1,0:T(1,128)} %broadcast_in_dim.97), calls=%async_computation.3 | async-start | bytes 131072 | tf_op jit(solution)/shard_map/all_to_all | solution.py:15
  75.9 21.5 %all-to-all-start.4 = ((bf16[32,24,384]{2,1,0:T(8,128)(2,1)}), bf16[32,24,384]{2,1,0:T(8,128)(2,1)S(1)}, u32[]{:S(2)}, u32[]{:S(2)}) async-start(bf16[32,24,384]{2,1,0:T(8,128)(2,1)} %broadcast_in_dim.98), calls=%async_computation.4 | async-start | bytes 1179648 | tf_op jit(solution)/shard_map/all_to_all | solution.py:15
  98.3 35.2 %all-to-all-start.5 = ((bf16[32,384,24]{1,2,0:T(8,128)(2,1)}), bf16[32,384,24]{1,2,0:T(8,128)(2,1)S(1)}, u32[]{:S(2)}, u32[]{:S(2)}) async-start(bf16[32,384,24]{1,2,0:T(8,128)(2,1)} %broadcast_in_dim.99), calls=%async_computation.5 | async-start | bytes 1179648 | tf_op jit(solution)/shard_map/all_to_all | solution.py:15
  136.7 27.7 %all-to-all-start.6 = ((bf16[8,1024,96]{1,2,0:T(8,128)(2,1)}), bf16[8,1024,96]{1,2,0:T(8,128)(2,1)S(1)}, u32[]{:S(2)}, u32[]{:S(2)}) async-start(bf16[8,1024,96]{1,2,0:T(8,128)(2,1)} %bitcast.279), calls=%async_computation.6 | async-start | bytes 3145728 | tf_op jit(solution)/shard_map/all_to_all | solution.py:82
  165.5 9.1 %all-to-all-start.7 = ((f32[8,1,2048]{2,1,0:T(1,128)}), f32[8,1,2048]{2,1,0:T(1,128)S(1)}, u32[]{:S(2)}, u32[]{:S(2)}) async-start(f32[8,1,2048]{2,1,0:T(1,128)} %broadcast_in_dim.100), calls=%async_computation.7 | async-start | bytes 131072 | tf_op jit(solution)/shard_map/all_to_all | solution.py:15
  176.9 20.7 %all-to-all-start.8 = ((bf16[2,192,8,32]{1,2,0,3:T(8,128)(2,1)}), bf16[2,192,8,32]{1,2,0,3:T(8,128)(2,1)S(1)}, u32[]{:S(2)}, u32[]{:S(2)}) async-start(bf16[2,192,8,32]{1,2,0,3:T(8,128)(2,1)} %copy.251), calls=%async_computation.8 | async-start | bytes 524288 | tf_op jit(solution)/shard_map/all_to_all | solution.py:34
  230.3 21.5 %all-to-all-start.11 = ((bf16[32,24,384]{2,1,0:T(8,128)(2,1)}), bf16[32,24,384]{2,1,0:T(8,128)(2,1)S(1)}, u32[]{:S(2)}, u32[]{:S(2)}) async-start(bf16[32,24,384]{2,1,0:T(8,128)(2,1)} %broadcast_in_dim.102), calls=%async_computation.11 | async-start | bytes 1179648 | tf_op jit(solution)/shard_map/all_to_all | solution.py:15
  252.7 35.4 %all-to-all-start.12 = ((bf16[32,384,24]{1,2,0:T(8,128)(2,1)}), bf16[32,384,24]{1,2,0:T(8,128)(2,1)}, u32[]{:S(2)}, u32[]{:S(2)}) async-start(bf16[32,384,24]{1,2,0:T(8,128)(2,1)} %broadcast_in_dim.103), calls=%async_computation.12 | async-start | bytes 1179648 | tf_op jit(solution)/shard_map/all_to_all | solution.py:15
where the time goes:
time: 322 us; the launch traced here: 321 us
  blocking collectives  113 us (35%)
  waiting for transfers between devices  96 us (30%)
  starting transfers between devices  68.2 us (21%)
  matrix products  18.4 us (6%)
  local copies, waits for them, and re-layouts  17.4 us (5%)
  other arithmetic  7.38 us (2%)
    all_gather x8, blocking collectives, stacked_from(): tiles = lax.all_gather(tiles, axes[k], axis=0, tiled=True)  59.3 us
    all_to_all x7, waiting for transfers between devices, from_everyone(): return lax.all_to_all(copies, axis, split_axis=0, concat_axis=0, tiled=True)  43.9 us
    all_to_all x7, starting transfers between devices, from_everyone(): return lax.all_to_all(copies, axis, split_axis=0, concat_axis=0, tiled=True)  36.8 us
    all_to_all x3, waiting for transfers between devices, sent_together(): lax.all_to_all(both, axis, split_axis=split_dim, concat_axis=concat_dim,...  32 us
    all_to_all x1, blocking collectives, summed_on_arrival(): lax.all_to_all(tiles, axis, split_axis=0, concat_axis=0, tiled=True)  27.6 us
    all_to_all x3, starting transfers between devices, sent_together(): lax.all_to_all(both, axis, split_axis=split_dim, concat_axis=concat_dim,...  24.3 us
    all_to_all x1, waiting for transfers between devices, summed_on_arrival(): lax.all_to_all(tiles, axis, split_axis=0, concat_axis=0, tiled=True)  20.1 us
    all_to_all x1, blocking collectives, sent_together(): lax.all_to_all(both, axis, split_axis=split_dim, concat_axis=concat_dim,...  14.9 us
  transfers between devices with their start and end apart: 11, of which 8 were waited for; matrix products, arithmetic and copies ran while one was open for 3% of the time, Pallas kernels for 0%

commit v1 on v0

v1 whole, which is shorter than its diff:
```python
import functools

import jax
import jax.numpy as jnp
import numpy as np
from jax import lax
from jax.experimental import pallas as pl
from jax.experimental.pallas import tpu as pltpu
from jax.sharding import PartitionSpec as P

MESH = pl.DeviceIdType.MESH
F32 = jnp.float32
BF16 = jnp.bfloat16

GRID = 64
LAYERS = 2
NR = 32
NC = 8
NZ, NY = 8, 4
CH = 96
OWN = 3
HID = 384
TAP = 24
PIX = 512
HALF = 256
EPS = 1e-06


def matrices():
    index = np.arange(GRID)
    angle = 2.0 * np.pi * ((index[:, None] * index[None, :]) % GRID) / GRID
    cosine, sine = np.cos(angle), np.sin(angle)
    pairs = np.eye(4)

    def first(table):
        return np.einsum("jh,pq->pjhq", table, pairs).reshape(HALF, HALF)

    def second(table):
        return np.kron(np.eye(2), table)

    forward_rows = np.concatenate([first(cosine), -first(sine)], axis=0)
    forward_lanes = np.block([[second(cosine), -second(sine)], [second(sine), second(cosine)]])
    inverse_lanes = np.block([[second(cosine), second(sine)], [-second(sine), second(cosine)]])
    inverse_rows = np.concatenate([first(cosine).T, -first(sine).T], axis=1)
    spread = np.zeros((HALF, HALF))
    for place in range(8):
        for c in range(32):
            spread[c * 8 + place, place * 32 + c] = 1.0
    return tuple(
        np.asarray(m, dtype=jnp.bfloat16)
        for m in (forward_rows, forward_lanes, inverse_lanes, inverse_rows, spread, spread.T)
    )


def dot(a, b):
    return jnp.dot(a, b, preferred_element_type=F32)


def arrived(ref, sem):
    pltpu.make_async_copy(ref, ref, sem).wait()


def kernel(
    tokens,
    spectral,
    gain_in,
    gain_mid,
    expand,
    bias,
    shrink,
    fwd_rows,
    fwd_lanes,
    inv_lanes,
    inv_rows,
    spread,
    gather,
    out,
    spec_buf,
    filt,
    small_rx,
    stats_rx,
    there_tx,
    there_rx,
    back_tx,
    back_rx,
    ag_tx,
    ag_rx,
    rs_tx,
    rs_rx,
    w_all,
    et,
    st,
    gcol,
    bcol,
    turn,
    spec_sem,
    small_s,
    small_r,
    stats_s,
    stats_r,
    there_s,
    there_r,
    back_s,
    back_r,
    ag_s,
    ag_r,
    rs_s,
    rs_r,
    wy_s,
    wy_r,
    wz_s,
    wz_r,
    wc_s,
    wc_r,
):
    r = lax.axis_index("rows")
    c = lax.axis_index("chan")
    z, y = r // NY, r % NY
    x, core = c // 2, c % 2

    barrier = pltpu.get_barrier_semaphore()

    def greet_row(t, carry):
        pl.semaphore_signal(barrier, inc=1, device_id=((r + t) % NR, c), device_id_type=MESH)
        return carry

    def greet_chan(t, carry):
        pl.semaphore_signal(barrier, inc=1, device_id=(r, (c + t) % NC), device_id_type=MESH)
        return carry

    lax.fori_loop(1, NC, greet_chan, 0)
    lax.fori_loop(1, NR, greet_row, 0)

    group = r // 8 * 8
    lane = r % 8

    def spec_copy(layer, i):
        start = pl.multiple_of(i * NR + group, 8)
        return pltpu.make_async_copy(
            spectral.at[layer, :, pl.ds(start, 8), :], spec_buf.at[layer, i], spec_sem.at[layer, i]
        )

    for layer in range(LAYERS):
        for i in range(OWN):
            spec_copy(layer, i).start()

    eye_tap = (
        lax.broadcasted_iota(jnp.int32, (TAP, TAP), 0)
        == lax.broadcasted_iota(jnp.int32, (TAP, TAP), 1)
    ).astype(F32).astype(BF16)
    for layer in range(LAYERS):
        w_all[layer, core, z, y, 0:3] = expand[layer].reshape(3, 8, HID)
        turned = lax.dot_general(
            eye_tap, shrink[layer], (((1,), (1,)), ((), ())), preferred_element_type=F32
        )
        w_all[layer, core, z, y, 3:6] = turned.astype(BF16).reshape(3, 8, HID)

    small_rx[c] = jnp.zeros((4, PIX), F32)
    turn[...] = jnp.zeros((128, 128), F32)
    small_rx[c, 0:2, 0:CH] = gain_mid[...]
    small_rx[c, 2:4, 0:HID] = bias[...].astype(F32)

    out[...] = tokens[...]

    def put_stats(layer):
        for hl in range(2):
            value = out[hl]
            stats_rx[layer, c, hl : hl + 1, :] = jnp.sum(value, axis=0, keepdims=True)
            stats_rx[layer, c, hl + 2 : hl + 3, :] = jnp.sum(value * value, axis=0, keepdims=True)

    def chan_copy(t, buf, send, recv):
        return pltpu.make_async_remote_copy(
            src_ref=buf.at[c],
            dst_ref=buf.at[c],
            send_sem=send,
            recv_sem=recv,
            device_id=(r, (c + t) % NC),
            device_id_type=MESH,
        )

    def send_all(buf, send, recv):
        def one(t, carry):
            chan_copy(t, buf, send, recv).start()
            return carry

        lax.fori_loop(1, NC, one, 0)

    put_stats(0)
    pl.semaphore_wait(barrier, NR - 1 + NC - 1)
    send_all(stats_rx.at[0], stats_s.at[0], stats_r.at[0])
    send_all(small_rx, small_s, small_r)

    def wy_copy(layer, t):
        ref = w_all.at[layer, core, z, y]
        return pltpu.make_async_remote_copy(
            src_ref=ref,
            dst_ref=ref,
            send_sem=wy_s.at[layer, t],
            recv_sem=wy_r.at[layer, t],
            device_id=(z * NY + (y + t) % NY, c),
            device_id_type=MESH,
        )

    def wz_ref(layer, step, way, mine):
        if mine:
            shift = step - 1
        else:
            shift = step
        at = (z + 2 * NZ - shift) % NZ if way == 0 else (z + shift) % NZ
        ref = w_all.at[layer, core, at]
        if step == 4:
            ref = ref.at[pl.ds(2 * way, 2)]
        return ref

    def wz_copy(layer, step, way):
        ref = wz_ref(layer, step, way, True)
        target = (z + 1) % NZ if way == 0 else (z + NZ - 1) % NZ
        return pltpu.make_async_remote_copy(
            src_ref=ref,
            dst_ref=ref,
            send_sem=wz_s.at[layer, step - 1, way],
            recv_sem=wz_r.at[layer, step - 1, way],
            device_id=(target * NY + y, c),
            device_id_type=MESH,
        )

    def wz_start(layer, step):
        for way in range(2):
            wz_copy(layer, step, way).start()

    def wz_wait(layer, step):
        for way in range(2):
            arrived(wz_ref(layer, step, way, False), wz_r.at[layer, step - 1, way])

    def wc_copy(layer):
        ref = w_all.at[layer, core]
        return pltpu.make_async_remote_copy(
            src_ref=ref,
            dst_ref=ref,
            send_sem=wc_s.at[layer],
            recv_sem=wc_r.at[layer],
            device_id=(r, x * 2 + 1 - core),
            device_id_type=MESH,
        )

    def wy_wait(layer):
        for t in range(1, NY):
            arrived(w_all.at[layer, core, z, (y + NY - t) % NY], wy_r.at[layer, t])

    for layer in range(LAYERS):
        for t in range(1, NY):
            wy_copy(layer, t).start()

    lanes = lax.broadcasted_iota(jnp.int32, (1, CH), 1)
    for layer in range(LAYERS):
        for i in range(OWN):
            spec_copy(layer, i).wait()
            values = spec_buf.at[layer, i].reshape(GRID * 8, 128)[pl.ds(lane, GRID, stride=8), :]
            gain = jnp.sum(
                jnp.where(lanes == i * NR + r, gain_in[layer : layer + 1, :], 0.0), axis=1, keepdims=True
            ) * (1.0 / (GRID * GRID))
            values = values * gain
            filt[layer, i] = jnp.concatenate([values, values], axis=0).T

    def exchange(tx, rx, send, recv):
        def one(t, carry):
            to = (r + t) % NR
            pltpu.make_async_remote_copy(
                src_ref=tx.at[to],
                dst_ref=rx.at[r],
                send_sem=send,
                recv_sem=recv,
                device_id=(to, c),
                device_id_type=MESH,
            ).start()
            return carry

        lax.fori_loop(1, NR, one, 0)
        pltpu.make_async_copy(tx.at[r], rx.at[r], recv).start()

    def as_matrix(rx):
        return jnp.concatenate(
            [rx[:, i].astype(F32).reshape(HALF, 128) for i in range(OWN)], axis=1
        ).astype(BF16)

    def from_matrix(tx, value):
        for i in range(OWN):
            tx[:, i] = value[:, i * 128 : (i + 1) * 128].reshape(NR, 8, 128).astype(BF16)

    def columns(layer):
        turn[0:8, :] = small_rx[:, layer, 0:128]
        value = turn[...].T
        for s in range(NC):
            gcol[layer, s * CH : (s + 1) * CH, :] = value[0:CH, s : s + 1]
        for k in range(2):
            for t in range(3):
                row = 3 * k + t
                turn[row : row + 1, :] = small_rx[2 * x + k, 2 + layer : 3 + layer, t * 128 : (t + 1) * 128]
        value = turn[...].T
        for row in range(6):
            bcol[layer, row * 128 : (row + 1) * 128, :] = value[:, row : row + 1]

    def weights(layer):
        for k in range(2):
            e = w_all[layer, k, :, :, 0:3].astype(F32).reshape(768, HID)
            et[layer, k * HID : (k + 1) * HID, :] = e.T.astype(BF16)
            s = w_all[layer, k, :, :, 3:6].astype(F32).reshape(768, HID)
            st[layer, :, k * HID : (k + 1) * HID] = s.astype(BF16)

    for layer in range(LAYERS):
        arrived(stats_rx.at[layer, pl.ds(0, NC - 1)], stats_r.at[layer])
        totals = jnp.sum(stats_rx[layer], axis=0)
        mean = totals[0:2] * (1.0 / 768.0)
        rstd = lax.rsqrt(totals[2:4] * (1.0 / 768.0) - mean * mean + EPS)
        pieces = []
        for hl in range(2):
            normed = ((out[hl] - mean[hl : hl + 1]) * rstd[hl : hl + 1]).astype(BF16)
            for pair in range(4):
                pieces.append(
                    jnp.concatenate(
                        [
                            normed[i * NR : (i + 1) * NR, pair * 128 : (pair + 1) * 128]
                            for i in range(OWN)
                        ],
                        axis=1,
                    )
                )
        from_matrix(there_tx.at[layer], dot(spread[...], jnp.concatenate(pieces, axis=0)))
        exchange(there_tx.at[layer], there_rx.at[layer], there_s.at[layer], there_r.at[layer])

        if layer == 0:
            arrived(small_rx.at[pl.ds(0, NC - 1)], small_r)
            wy_wait(0)
            wz_start(0, 1)
            columns(0)
            columns(1)
        else:
            wz_wait(1, 4)
            wc_copy(1).start()

        arrived(there_rx.at[layer], there_r.at[layer])
        a = dot(fwd_rows[...], as_matrix(there_rx.at[layer])).astype(BF16)
        reals, imags = [], []
        for i in range(OWN):
            at = slice(i * 128, (i + 1) * 128)
            b = dot(jnp.concatenate([a[:HALF, at], a[HALF:, at]], axis=1), fwd_lanes[...])
            b_re = b[:, :128].reshape(4, GRID, 128)
            b_im = b[:, 128:].reshape(4, GRID, 128)
            f_re = filt[layer, i, 0:GRID][None]
            f_im = filt[layer, i, GRID:][None]
            c_re = (b_re * f_re - b_im * f_im).reshape(HALF, 128)
            c_im = (b_re * f_im + b_im * f_re).reshape(HALF, 128)
            e = dot(jnp.concatenate([c_re, c_im], axis=1).astype(BF16), inv_lanes[...]).astype(BF16)
            reals.append(e[:, :128])
            imags.append(e[:, 128:])
        both = jnp.concatenate(
            [jnp.concatenate(reals, axis=1), jnp.concatenate(imags, axis=1)], axis=0
        )
        from_matrix(back_tx.at[layer], dot(inv_rows[...], both))
        exchange(back_tx.at[layer], back_rx.at[layer], back_s.at[layer], back_r.at[layer])

        if layer == 0:
            wz_wait(0, 1)
            wz_start(0, 2)
        else:
            arrived(w_all.at[1, 1 - core], wc_r.at[1])
            weights(1)

        arrived(back_rx.at[layer], back_r.at[layer])
        mixed = dot(gather[...], as_matrix(back_rx.at[layer])).astype(BF16)
        for hl in range(2):
            for pair in range(4):
                row = (hl * 4 + pair) * NR
                for i in range(OWN):
                    ag_tx[
                        layer,
                        hl,
                        pair // 2,
                        i * NR : (i + 1) * NR,
                        (pair % 2) * 128 : (pair % 2 + 1) * 128,
                    ] = mixed[row : row + NR, i * 128 : (i + 1) * 128]

        for half in range(2):

            def share(t, carry, half=half):
                to = (c + t) % NC
                pltpu.make_async_remote_copy(
                    src_ref=ag_tx.at[layer, to % 2, half],
                    dst_ref=ag_rx.at[layer, half, c],
                    send_sem=ag_s.at[layer, half],
                    recv_sem=ag_r.at[layer, half],
                    device_id=(r, to),
                    device_id_type=MESH,
                ).start()
                return carry

            lax.fori_loop(1, NC, share, 0)
            pltpu.make_async_copy(
                ag_tx.at[layer, core, half], ag_rx.at[layer, half, c], ag_r.at[layer, half]
            ).start()

        if layer == 0:
            wz_wait(0, 2)
            wz_start(0, 3)
            wz_wait(0, 3)
            wz_start(0, 4)
            wz_wait(0, 4)
            wc_copy(0).start()
            wy_wait(1)
            wz_start(1, 1)
            arrived(w_all.at[0, 1 - core], wc_r.at[0])
            weights(0)

        for half in range(2):
            arrived(ag_rx.at[layer, half], ag_r.at[layer, half])
            value = ag_rx[layer, half].astype(F32).reshape(768, HALF)
            mean = jnp.sum(value, axis=0, keepdims=True) * (1.0 / 768.0)
            square = jnp.sum(value * value, axis=0, keepdims=True) * (1.0 / 768.0)
            rstd = lax.rsqrt(square - mean * mean + EPS)
            normed2 = ((value - mean) * rstd * gcol[layer]).astype(BF16)
            hidden = jax.nn.gelu(dot(et[layer], normed2) + bcol[layer], approximate=True)
            part = dot(st[layer], hidden.astype(BF16))
            rs_tx[layer, half] = part.astype(BF16).reshape(NC, CH, HALF)

            def give(t, carry, half=half):
                to = (c + t) % NC
                pltpu.make_async_remote_copy(
                    src_ref=rs_tx.at[layer, half, to],
                    dst_ref=rs_rx.at[layer, half, c],
                    send_sem=rs_s.at[layer, half],
                    recv_sem=rs_r.at[layer, half],
                    device_id=(r, to),
                    device_id_type=MESH,
                ).start()
                return carry

            lax.fori_loop(1, NC, give, 0)
            pltpu.make_async_copy(
                rs_tx.at[layer, half, c], rs_rx.at[layer, half, c], rs_r.at[layer, half]
            ).start()

        if layer == 0:
            wz_wait(1, 1)
            wz_start(1, 2)
            wz_wait(1, 2)
            wz_start(1, 3)

        for half in range(2):
            arrived(rs_rx.at[layer, half], rs_r.at[layer, half])
            at = slice(half * HALF, (half + 1) * HALF)
            for hl in range(2):
                total = rs_rx[layer, half, hl].astype(F32)
                for chip in range(1, 4):
                    total = total + rs_rx[layer, half, 2 * chip + hl].astype(F32)
                out[hl, :, at] = out[hl, :, at] + total.astype(BF16).astype(F32)

        if layer == 0:
            put_stats(1)
            send_all(stats_rx.at[1], stats_s.at[1], stats_r.at[1])
            wz_wait(1, 3)
            wz_start(1, 4)

    arrived(small_rx.at[pl.ds(0, NC - 1)], small_s)
    for layer in range(LAYERS):
        arrived(stats_rx.at[layer, pl.ds(0, NC - 1)], stats_s.at[layer])
        arrived(there_tx.at[layer, pl.ds(0, NR - 1)], there_s.at[layer])
        arrived(back_tx.at[layer, pl.ds(0, NR - 1)], back_s.at[layer])
        for half in range(2):
            arrived(ag_rx.at[layer, half, pl.ds(0, NC - 1)], ag_s.at[layer, half])
            arrived(rs_rx.at[layer, half, pl.ds(0, NC - 1)], rs_s.at[layer, half])
        for t in range(1, NY):
            wy_copy(layer, t).wait_send()
        for step in range(1, 5):
            for way in range(2):
                wz_copy(layer, step, way).wait_send()
        wc_copy(layer).wait_send()


def per_device(tokens, spectral, gain_in, gain_mid, expand, bias, shrink):
    vmem = pl.BlockSpec(memory_space=pltpu.VMEM)
    dma = pltpu.SemaphoreType.DMA
    tables = [jnp.asarray(m) for m in matrices()]
    return pl.pallas_call(
        kernel,
        out_shape=jax.ShapeDtypeStruct(tokens.shape, F32),
        in_specs=[vmem, pl.BlockSpec(memory_space=pl.ANY)] + [vmem] * 11,
        out_specs=vmem,
        scratch_shapes=[
            pltpu.VMEM((LAYERS, OWN, GRID, 8, 128), F32),
            pltpu.VMEM((LAYERS, OWN, 128, 128), F32),
            pltpu.VMEM((NC, 4, PIX), F32),
            pltpu.VMEM((LAYERS, NC, 4, PIX), F32),
            pltpu.VMEM((LAYERS, NR, OWN, 8, 128), BF16),
            pltpu.VMEM((LAYERS, NR, OWN, 8, 128), BF16),
            pltpu.VMEM((LAYERS, NR, OWN, 8, 128), BF16),
            pltpu.VMEM((LAYERS, NR, OWN, 8, 128), BF16),
            pltpu.VMEM((LAYERS, 2, 2, CH, HALF), BF16),
            pltpu.VMEM((LAYERS, 2, NC, CH, HALF), BF16),
            pltpu.VMEM((LAYERS, 2, NC, CH, HALF), BF16),
            pltpu.VMEM((LAYERS, 2, NC, CH, HALF), BF16),
            pltpu.VMEM((LAYERS, 2, NZ, NY, 6, 8, HID), BF16),
            pltpu.VMEM((LAYERS, 768, 768), BF16),
            pltpu.VMEM((LAYERS, 768, 768), BF16),
            pltpu.VMEM((LAYERS, 768, 1), F32),
            pltpu.VMEM((LAYERS, 768, 1), F32),
            pltpu.VMEM((128, 128), F32),
            dma((LAYERS, OWN)),
            dma(()),
            dma(()),
            dma((LAYERS,)),
            dma((LAYERS,)),
            dma((LAYERS,)),
            dma((LAYERS,)),
            dma((LAYERS,)),
            dma((LAYERS,)),
            dma((LAYERS, 2)),
            dma((LAYERS, 2)),
            dma((LAYERS, 2)),
            dma((LAYERS, 2)),
            dma((LAYERS, NY)),
            dma((LAYERS, NY)),
            dma((LAYERS, 4, 2)),
            dma((LAYERS, 4, 2)),
            dma((LAYERS,)),
            dma((LAYERS,)),
        ],
        compiler_params=pltpu.CompilerParams(
            collective_id=0, has_side_effects=True, vmem_limit_bytes=56 * 1024 * 1024
        ),
        name="blocks",
    )(tokens, spectral, gain_in, gain_mid, expand, bias, shrink, *tables)


def solution(mesh):
    placed = (
        P("rows", "chan", None),
        P(None, None, "chan", None),
        P(None, "chan"),
        P(None, "chan"),
        P(None, "rows", "chan"),
        P(None, "chan"),
        P(None, "chan", "rows"),
    )
    return jax.shard_map(
        per_device, mesh=mesh, in_specs=placed, out_specs=P("rows", "chan", None), check_vma=False
    )
```

time: 322 us -> 106 us (0.33)
  blocking collectives: 113 us -> 0 us
  Pallas kernels: 0 us -> 103 us
  waiting for transfers between devices: 96 us -> 0 us
  starting transfers between devices: 68.2 us -> 0 us
  matrix products: 18.4 us -> 0 us
  local copies, waits for them, and re-layouts: 17.4 us -> 3.35 us
  other arithmetic: 7.38 us -> 0 us
    pallas_call x0 -> x1, Pallas kernels: none -> 103 us  [per_device(): pl.pallas_call(kernel, out_shape=jax.ShapeDtypeStruct(tokens.shape, F32),...]
    all_to_all x11 -> x0, waiting for transfers between devices: 96 us -> none  [the longest x7 43.9 us: from_everyone(): return lax.all_to_all(copies, axis, split_axis=0, concat_axis=0, tiled=True)]
    all_to_all x11 -> x0, starting transfers between devices: 68.2 us -> none  [the longest x7 36.8 us: from_everyone(): return lax.all_to_all(copies, axis, split_axis=0, concat_axis=0, tiled=True)]
    all_gather x8 -> x0, blocking collectives: 59.3 us -> none  [stacked_from(): tiles = lax.all_gather(tiles, axes[k], axis=0, tiled=True)]
    all_to_all x3 -> x0, blocking collectives: 53.5 us -> none  [the longest x1 27.6 us: summed_on_arrival(): lax.all_to_all(tiles, axis, split_axis=0, concat_axis=0, tiled=True)]
    dot_general x26 -> x0, matrix products: 18.4 us -> none  [the longest x2 7.37 us: per_device(): jnp.dot(hidden, gather_directly(shrink[layer], 'rows', 1), preferred_elem...]
    broadcast_in_dim x8 -> x0, local copies, waits for them, and re-layouts: 5.53 us -> none  [from_everyone(): copies = jnp.broadcast_to(value, (lax.axis_size(axis), *value.shape))]
    squeeze x4 -> x0, local copies, waits for them, and re-layouts: 4.23 us -> none  [the longest x1 3.33 us: per_device(): spec_layer = spectral[layer]]
  transfers between devices with their start and end apart: 11 -> 0, of which waited for: 8 -> 0; matrix products, arithmetic and copies ran while one was open for 3% -> 0% of each run, Pallas kernels for 0% -> 0%
where the time goes in v1:
time: 106 us
  Pallas kernels  103 us (97%)
  local copies, waits for them, and re-layouts  3.35 us (3%)
    pallas_call x1, Pallas kernels, per_device(): pl.pallas_call(kernel, out_shape=jax.ShapeDtypeStruct(tokens.shape, F32),...  103 us
    unnamed x2, local copies, waits for them, and re-layouts  3.35 us

profile of v1, /device:TPU:1, one launch (start us, length us, event | category | flops | bytes accessed | tf_op | source)
XLA Modules:
  0.0 106.3 jit_solution(12771782594212202587)
XLA Ops:
  0.0 1.6 %copy.14.shrink = bf16[2,384,24]{2,1,0:T(8,128)(2,1)} copy(bf16[2,384,24]{1,2,0:T(8,128)(2,1)} %param.19) | data formatting | bytes 73728 | tf_op args[6]
  1.6 102.9 %blocks.1 = f32[2,96,512]{2,1,0:T(8,128)} custom-call(f32[2,96,512]{2,1,0:T(8,128)} %tokens.1, f32[2,64,96,128]{3,2,1,0:T(8,128)} %spectral.1, f32[2,96]{1,0:T(2,128)} %gain_in.1, f32[2,96]{1,0:T(2,128)} %gain_mid.1, bf16[2,24,384]{2,1,0:T(8,128)(2,1)} %expand.1, bf16[2,384]{1,0:T(2,128)(2,1)} %bias.1, bf16[2,384,24]{2,1,0:T(8,128)(2,1)} %copy.14.shrink, ...), custom_call_target="tpu_custom_call" | custom-call | tf_op jit(solution)/shard_map/blocks/pallas_call | solution.py:483
  104.5 1.8 %copy.16 = f32[2,96,512]{2,1,0:T(8,128)} copy(f32[2,96,512]{2,1,0:T(8,128)} %blocks.1) | data formatting | bytes 786432

commit v2 on v0

v2 whole, which is shorter than its diff:
```python
import functools

import jax
import jax.numpy as jnp
import numpy as np
from jax import lax
from jax.experimental import pallas as pl
from jax.experimental.pallas import tpu as pltpu
from jax.sharding import PartitionSpec as P

MESH = pl.DeviceIdType.MESH
F32 = jnp.float32
BF16 = jnp.bfloat16

GRID = 64
LAYERS = 2
NR = 32
NC = 8
NZ, NY = 8, 4
CH = 96
OWN = 3
HID = 384
PIX = 512
NS = 2
WIDE = PIX // NS
PAIRS = WIDE // 128
PLACES = 2 * PAIRS
DEPTH = NR * PLACES
EPS = 1e-06
STOP = None


def matrices():
    index = np.arange(GRID)
    angle = 2.0 * np.pi * ((index[:, None] * index[None, :]) % GRID) / GRID
    cosine, sine = np.cos(angle), np.sin(angle)
    pairs = np.eye(PAIRS)

    def first(table):
        return np.einsum("jh,pq->pjhq", table, pairs).reshape(DEPTH, DEPTH)

    def second(table):
        return np.kron(np.eye(2), table)

    forward_rows = np.concatenate([first(cosine), -first(sine)], axis=0)
    forward_lanes = np.block([[second(cosine), -second(sine)], [second(sine), second(cosine)]])
    inverse_lanes = np.block([[second(cosine), second(sine)], [-second(sine), second(cosine)]])
    inverse_rows = np.concatenate([first(cosine).T, -first(sine).T], axis=1)
    spread = np.zeros((DEPTH, DEPTH))
    for place in range(PLACES):
        for c in range(NR):
            spread[c * PLACES + place, place * NR + c] = 1.0
    return tuple(
        np.asarray(m, dtype=jnp.bfloat16)
        for m in (forward_rows, forward_lanes, inverse_lanes, inverse_rows, spread, spread.T)
    )


def dot(a, b):
    return jnp.dot(a, b, preferred_element_type=F32)


def arrived(ref, sem):
    pltpu.make_async_copy(ref, ref, sem).wait()


def kernel(*refs):
    (
        (tokens, spectral, gain_in, gain_mid, expand, bias, shrink),
        table_hbm,
        (out,),
        table,
        (gi_buf, gm_buf, b_buf, spec_buf, filt, small_rx, stats_rx),
        (there_tx, there_rx, back_tx, back_rx, ag_tx, ag_rx, rs_tx, rs_rx),
        (w_all, et, st, gcol, bcol, turn),
        (in_sem, spec_sem, small_s, small_r, stats_s, stats_r, there_s, there_r, back_s, back_r),
        (ag_s, ag_r, rs_s, rs_r, wy_s, wy_r, wz_s, wz_r, wc_s, wc_r),
    ) = [
        tuple(refs[a:b])
        for a, b in zip((0, 7, 13, 14, 20, 27, 35, 41, 51), (7, 13, 14, 20, 27, 35, 41, 51, 61))
    ]
    fwd_rows, fwd_lanes, inv_lanes, inv_rows, spread, gather = table

    r = lax.axis_index("rows")
    c = lax.axis_index("chan")
    z, y = r // NY, r % NY
    x, core = c // 2, c % 2

    pending = {}
    leaving = []

    def owed(key):
        pending.pop(key)()

    def wait(*key):
        return lambda: owed(key)


    barrier = pltpu.get_barrier_semaphore()

    def greet_row(t, carry):
        pl.semaphore_signal(barrier, inc=1, device_id=((r + t) % NR, c), device_id_type=MESH)
        return carry

    def greet_chan(t, carry):
        pl.semaphore_signal(barrier, inc=1, device_id=(r, (c + t) % NC), device_id_type=MESH)
        return carry

    def spec_copy(layer, i):
        start = pl.multiple_of(i * NR + r // 8 * 8, 8)
        return pltpu.make_async_copy(
            spectral.at[layer, :, pl.ds(start, 8), :], spec_buf.at[layer, i], spec_sem.at[layer, i]
        )

    loads = [
        (tokens, out),
        (gain_in, gi_buf),
        (gain_mid, gm_buf),
        (bias, b_buf),
        *zip(table_hbm, table),
    ]
    for layer in range(LAYERS):
        own = w_all.at[layer, core, z, y]
        loads.append((expand.at[layer], own.at[pl.ds(0, 3)]))
        loads.append((shrink.at[layer], own.at[pl.ds(3, 3)]))
    loads = [pltpu.make_async_copy(a, b, in_sem.at[k]) for k, (a, b) in enumerate(loads)]

    def put_stats(layer, s):
        at = slice(s * WIDE, (s + 1) * WIDE)
        for hl in range(2):
            value = out[hl, :, at]
            stats_rx[layer, s, c, hl : hl + 1, :] = jnp.sum(value, axis=0, keepdims=True)
            stats_rx[layer, s, c, hl + 2 : hl + 3, :] = jnp.sum(value * value, axis=0, keepdims=True)

    def to_all(key, source, target, send, recv, whole):
        def one(t, carry):
            to = (c + t) % NC
            pltpu.make_async_remote_copy(
                src_ref=source(to),
                dst_ref=target.at[c],
                send_sem=send,
                recv_sem=recv,
                device_id=(r, to),
                device_id_type=MESH,
            ).start()
            return carry

        lax.fori_loop(1, NC, one, 0)
        if whole:
            pltpu.make_async_copy(source(c), target.at[c], recv).start()
            pending[key] = lambda: arrived(target, recv)
        else:
            pending[key] = lambda: arrived(target.at[pl.ds(0, NC - 1)], recv)
        leaving.append(lambda: arrived(target.at[pl.ds(0, NC - 1)], send))

    def send_stats(layer, s):
        put_stats(layer, s)
        buf = stats_rx.at[layer, s]
        to_all(
            ("stats", layer, s), lambda to: buf.at[c], buf, stats_s.at[layer, s], stats_r.at[layer, s], False
        )

    def enter():
        lax.fori_loop(1, NC, greet_chan, 0)
        lax.fori_loop(1, NR, greet_row, 0)
        for copy in loads:
            copy.start()
        for layer in range(LAYERS):
            for i in range(OWN):
                spec_copy(layer, i).start()
        small_rx[c] = jnp.zeros((4, PIX), F32)
        turn[...] = jnp.zeros((128, 128), F32)
        for copy in loads:
            copy.wait()
        small_rx[c, 0:2, 0:CH] = gm_buf[...]
        small_rx[c, 2:4, 0:HID] = b_buf[...].astype(F32)
        pl.semaphore_wait(barrier, NR - 1 + NC - 1)

    def send_small():
        to_all("small", lambda to: small_rx.at[c], small_rx, small_s, small_r, False)

    def filters():
        lanes = lax.broadcasted_iota(jnp.int32, (1, CH), 1)
        for layer in range(LAYERS):
            for i in range(OWN):
                spec_copy(layer, i).wait()
                values = spec_buf.at[layer, i].reshape(GRID * 8, 128)[pl.ds(r % 8, GRID, stride=8), :]
                gain = jnp.sum(
                    jnp.where(lanes == i * NR + r, gi_buf[layer : layer + 1, :], 0.0),
                    axis=1,
                    keepdims=True,
                ) * (1.0 / (GRID * GRID))
                values = values * gain
                filt[layer, i] = jnp.concatenate([values, values], axis=0).T

    def columns():
        owed("small")
        for layer in range(LAYERS):
            turn[0:8, :] = small_rx[:, layer, 0:128]
            value = turn[...].T
            for k in range(NC):
                gcol[layer, k * CH : (k + 1) * CH, :] = value[0:CH, k : k + 1]
            for k in range(2):
                for t in range(3):
                    row = 3 * k + t
                    turn[row : row + 1, :] = small_rx[
                        2 * x + k, 2 + layer : 3 + layer, t * 128 : (t + 1) * 128
                    ]
            value = turn[...].T
            for row in range(6):
                bcol[layer, row * 128 : (row + 1) * 128, :] = value[:, row : row + 1]


    def move(ref, send, recv, to, key, expected):
        copy = pltpu.make_async_remote_copy(
            src_ref=ref, dst_ref=ref, send_sem=send, recv_sem=recv, device_id=to, device_id_type=MESH
        )
        copy.start()
        leaving.append(copy.wait_send)
        earlier = pending.get(key)

        def done():
            if earlier is not None:
                earlier()
            arrived(expected, recv)

        pending[key] = done

    def wy(layer):
        ref = w_all.at[layer, core, z, y]
        for t in range(1, NY):
            move(
                ref,
                wy_s.at[layer, t],
                wy_r.at[layer, t],
                (z * NY + (y + t) % NY, c),
                ("w", layer, 0),
                w_all.at[layer, core, z, (y + NY - t) % NY],
            )

    def wz_ref(layer, step, way, shift):
        at = (z + 2 * NZ - shift) % NZ if way == 0 else (z + shift) % NZ
        ref = w_all.at[layer, core, at]
        return ref.at[pl.ds(2 * way, 2)] if step == 4 else ref

    def wz(layer, step):
        if ("w", layer, step - 1) in pending:
            owed(("w", layer, step - 1))
        for way in range(2):
            to = (z + 1) % NZ if way == 0 else (z + NZ - 1) % NZ
            move(
                wz_ref(layer, step, way, step - 1),
                wz_s.at[layer, step - 1, way],
                wz_r.at[layer, step - 1, way],
                (to * NY + y, c),
                ("w", layer, step),
                wz_ref(layer, step, way, step),
            )

    def wc(layer):
        owed(("w", layer, 4))
        move(
            w_all.at[layer, core],
            wc_s.at[layer],
            wc_r.at[layer],
            (r, x * 2 + 1 - core),
            ("w", layer, 5),
            w_all.at[layer, 1 - core],
        )

    def weights(layer):
        owed(("w", layer, 5))
        for k in range(2):
            e = w_all[layer, k, :, :, 0:3].astype(F32).reshape(768, HID)
            et[layer, k * HID : (k + 1) * HID, :] = e.T.astype(BF16)
            s = w_all[layer, k, :, :, 3:6].astype(F32).reshape(768, HID)
            st[layer, :, k * HID : (k + 1) * HID] = s.astype(BF16)


    def exchange(key, tx, rx, send, recv):
        def one(t, carry):
            to = (r + t) % NR
            pltpu.make_async_remote_copy(
                src_ref=tx.at[to],
                dst_ref=rx.at[r],
                send_sem=send,
                recv_sem=recv,
                device_id=(to, c),
                device_id_type=MESH,
            ).start()
            return carry

        lax.fori_loop(1, NR, one, 0)
        pltpu.make_async_copy(tx.at[r], rx.at[r], recv).start()
        pending[key] = lambda: arrived(rx, recv)
        leaving.append(lambda: arrived(tx.at[pl.ds(0, NR - 1)], send))

    def as_matrix(rx):
        return jnp.concatenate(
            [rx[:, i].astype(F32).reshape(DEPTH, 128) for i in range(OWN)], axis=1
        ).astype(BF16)

    def from_matrix(tx, value):
        for i in range(OWN):
            tx[:, i] = value[:, i * 128 : (i + 1) * 128].reshape(NR, PLACES, 128).astype(BF16)

    def there(layer, s):
        owed(("stats", layer, s))
        totals = jnp.sum(stats_rx[layer, s], axis=0)
        mean = totals[0:2] * (1.0 / 768.0)
        rstd = lax.rsqrt(totals[2:4] * (1.0 / 768.0) - mean * mean + EPS)
        pieces = []
        for hl in range(2):
            value = out[hl, :, s * WIDE : (s + 1) * WIDE]
            normed = ((value - mean[hl : hl + 1]) * rstd[hl : hl + 1]).astype(BF16)
            for pair in range(PAIRS):
                pieces.append(
                    jnp.concatenate(
                        [
                            normed[i * NR : (i + 1) * NR, pair * 128 : (pair + 1) * 128]
                            for i in range(OWN)
                        ],
                        axis=1,
                    )
                )
        tx = there_tx.at[layer, s]
        from_matrix(tx, dot(spread[...], jnp.concatenate(pieces, axis=0)))
        exchange(
            ("there", layer, s), tx, there_rx.at[layer, s], there_s.at[layer, s], there_r.at[layer, s]
        )

    def transform(layer, s):
        owed(("there", layer, s))
        a = dot(fwd_rows[...], as_matrix(there_rx.at[layer, s])).astype(BF16)
        reals, imags = [], []
        for i in range(OWN):
            at = slice(i * 128, (i + 1) * 128)
            b = dot(jnp.concatenate([a[:DEPTH, at], a[DEPTH:, at]], axis=1), fwd_lanes[...])
            b_re = b[:, :128].reshape(PAIRS, GRID, 128)
            b_im = b[:, 128:].reshape(PAIRS, GRID, 128)
            f_re = filt[layer, i, 0:GRID][None]
            f_im = filt[layer, i, GRID:][None]
            c_re = (b_re * f_re - b_im * f_im).reshape(DEPTH, 128)
            c_im = (b_re * f_im + b_im * f_re).reshape(DEPTH, 128)
            e = dot(jnp.concatenate([c_re, c_im], axis=1).astype(BF16), inv_lanes[...]).astype(BF16)
            reals.append(e[:, :128])
            imags.append(e[:, 128:])
        both = jnp.concatenate(
            [jnp.concatenate(reals, axis=1), jnp.concatenate(imags, axis=1)], axis=0
        )
        tx = back_tx.at[layer, s]
        from_matrix(tx, dot(inv_rows[...], both))
        exchange(
            ("back", layer, s), tx, back_rx.at[layer, s], back_s.at[layer, s], back_r.at[layer, s]
        )

    def share(layer, s):
        owed(("back", layer, s))
        mixed = dot(gather[...], as_matrix(back_rx.at[layer, s])).astype(BF16)
        for hl in range(2):
            for pair in range(PAIRS):
                row = (hl * PAIRS + pair) * NR
                for i in range(OWN):
                    ag_tx[layer, s, hl, i * NR : (i + 1) * NR, pair * 128 : (pair + 1) * 128] = mixed[
                        row : row + NR, i * 128 : (i + 1) * 128
                    ]
        to_all(
            ("ag", layer, s),
            lambda to: ag_tx.at[layer, s, to % 2],
            ag_rx.at[layer, s],
            ag_s.at[layer, s],
            ag_r.at[layer, s],
            True,
        )

    def mlp(layer, s):
        owed(("ag", layer, s))
        value = ag_rx[layer, s].astype(F32).reshape(768, WIDE)
        mean = jnp.sum(value, axis=0, keepdims=True) * (1.0 / 768.0)
        square = jnp.sum(value * value, axis=0, keepdims=True) * (1.0 / 768.0)
        rstd = lax.rsqrt(square - mean * mean + EPS)
        normed2 = ((value - mean) * rstd * gcol[layer]).astype(BF16)
        hidden = jax.nn.gelu(dot(et[layer], normed2) + bcol[layer], approximate=True)
        part = dot(st[layer], hidden.astype(BF16))
        rs_tx[layer, s] = part.astype(BF16).reshape(NC, CH, WIDE)
        to_all(
            ("rs", layer, s),
            lambda to: rs_tx.at[layer, s, to],
            rs_rx.at[layer, s],
            rs_s.at[layer, s],
            rs_r.at[layer, s],
            True,
        )

    def add(layer, s):
        owed(("rs", layer, s))
        at = slice(s * WIDE, (s + 1) * WIDE)
        for hl in range(2):
            total = rs_rx[layer, s, hl].astype(F32)
            for chip in range(1, 4):
                total = total + rs_rx[layer, s, 2 * chip + hl].astype(F32)
            out[hl, :, at] = out[hl, :, at] + total.astype(BF16).astype(F32)
        if layer + 1 < LAYERS:
            send_stats(layer + 1, s)


    plan = [("enter", enter)]

    def then(name, f, *args):
        plan.append((f"{name} {args}", functools.partial(f, *args)))

    def each(name, f, layer):
        for s in range(NS):
            then(name, f, layer, s)

    each("stats", send_stats, 0)
    then("wy", wy, 0)
    then("small", send_small)
    then("filters", filters)
    then("wz", wz, 0, 1)
    each("there", there, 0)
    then("columns", columns)
    each("transform", transform, 0)
    then("wz", wz, 0, 2)
    then("wy", wy, 1)
    each("share", share, 0)
    then("wz", wz, 0, 3)
    then("wz", wz, 0, 4)
    then("wc", wc, 0)
    then("wz", wz, 1, 1)
    then("weights", weights, 0)
    each("mlp", mlp, 0)
    then("wz", wz, 1, 2)
    then("wz", wz, 1, 3)
    each("add", add, 0)
    then("wz", wz, 1, 4)
    each("there", there, 1)
    then("wc", wc, 1)
    each("transform", transform, 1)
    then("weights", weights, 1)
    each("share", share, 1)
    each("mlp", mlp, 1)
    each("add", add, 1)

    for _, step in plan[:STOP]:
        step()
    for key in list(pending):
        owed(key)
    for done in leaving:
        done()


def per_device(tokens, spectral, gain_in, gain_mid, expand, bias, shrink):
    hbm = pl.BlockSpec(memory_space=pl.ANY)
    dma = pltpu.SemaphoreType.DMA
    tables = [jnp.asarray(m) for m in matrices()]
    message = (LAYERS, NS, NR, OWN, PLACES, 128)
    scratch = [pltpu.VMEM(m.shape, BF16) for m in tables]
    scratch += [
        pltpu.VMEM((LAYERS, CH), F32),
        pltpu.VMEM((LAYERS, CH), F32),
        pltpu.VMEM((LAYERS, HID), BF16),
        pltpu.VMEM((LAYERS, OWN, GRID, 8, 128), F32),
        pltpu.VMEM((LAYERS, OWN, 128, 128), F32),
        pltpu.VMEM((NC, 4, PIX), F32),
        pltpu.VMEM((LAYERS, NS, NC, 4, WIDE), F32),
        pltpu.VMEM(message, BF16),
        pltpu.VMEM(message, BF16),
        pltpu.VMEM(message, BF16),
        pltpu.VMEM(message, BF16),
        pltpu.VMEM((LAYERS, NS, 2, CH, WIDE), BF16),
        pltpu.VMEM((LAYERS, NS, NC, CH, WIDE), BF16),
        pltpu.VMEM((LAYERS, NS, NC, CH, WIDE), BF16),
        pltpu.VMEM((LAYERS, NS, NC, CH, WIDE), BF16),
        pltpu.VMEM((LAYERS, 2, NZ, NY, 6, 8, HID), BF16),
        pltpu.VMEM((LAYERS, 768, 768), BF16),
        pltpu.VMEM((LAYERS, 768, 768), BF16),
        pltpu.VMEM((LAYERS, 768, 1), F32),
        pltpu.VMEM((LAYERS, 768, 1), F32),
        pltpu.VMEM((128, 128), F32),
        dma((14,)),
        dma((LAYERS, OWN)),
        dma(()),
        dma(()),
    ]
    scratch += [dma((LAYERS, NS))] * 10
    scratch += [dma((LAYERS, NY))] * 2 + [dma((LAYERS, 4, 2))] * 2 + [dma((LAYERS,))] * 2
    return pl.pallas_call(
        kernel,
        out_shape=jax.ShapeDtypeStruct(tokens.shape, F32),
        in_specs=[hbm] * 13,
        out_specs=pl.BlockSpec(memory_space=pltpu.VMEM),
        scratch_shapes=scratch,
        compiler_params=pltpu.CompilerParams(
            collective_id=0, has_side_effects=True, vmem_limit_bytes=56 * 1024 * 1024
        ),
        name="blocks",
    )(
        tokens,
        spectral,
        gain_in,
        gain_mid,
        expand.reshape(LAYERS, 3, 8, HID),
        bias,
        shrink.transpose(0, 2, 1).reshape(LAYERS, 3, 8, HID),
        *tables,
    )


def solution(mesh):
    placed = (
        P("rows", "chan", None),
        P(None, None, "chan", None),
        P(None, "chan"),
        P(None, "chan"),
        P(None, "rows", "chan"),
        P(None, "chan"),
        P(None, "chan", "rows"),
    )
    return jax.shard_map(
        per_device, mesh=mesh, in_specs=placed, out_specs=P("rows", "chan", None), check_vma=False
    )
```

time: 322 us -> 100 us (0.31)
  blocking collectives: 113 us -> 0 us
  Pallas kernels: 0 us -> 98.1 us
  waiting for transfers between devices: 96 us -> 0 us
  starting transfers between devices: 68.2 us -> 0 us
  matrix products: 18.4 us -> 0 us
  local copies, waits for them, and re-layouts: 17.4 us -> 1.77 us
  other arithmetic: 7.38 us -> 0 us
    pallas_call x0 -> x1, Pallas kernels: none -> 98.1 us  [per_device(): pl.pallas_call(kernel, out_shape=jax.ShapeDtypeStruct(tokens.shape, F32),...]
    all_to_all x11 -> x0, waiting for transfers between devices: 96 us -> none  [the longest x7 43.9 us: from_everyone(): return lax.all_to_all(copies, axis, split_axis=0, concat_axis=0, tiled=True)]
    all_to_all x11 -> x0, starting transfers between devices: 68.2 us -> none  [the longest x7 36.8 us: from_everyone(): return lax.all_to_all(copies, axis, split_axis=0, concat_axis=0, tiled=True)]
    all_gather x8 -> x0, blocking collectives: 59.3 us -> none  [stacked_from(): tiles = lax.all_gather(tiles, axes[k], axis=0, tiled=True)]
    all_to_all x3 -> x0, blocking collectives: 53.5 us -> none  [the longest x1 27.6 us: summed_on_arrival(): lax.all_to_all(tiles, axis, split_axis=0, concat_axis=0, tiled=True)]
    dot_general x26 -> x0, matrix products: 18.4 us -> none  [the longest x2 7.37 us: per_device(): jnp.dot(hidden, gather_directly(shrink[layer], 'rows', 1), preferred_elem...]
    broadcast_in_dim x8 -> x0, local copies, waits for them, and re-layouts: 5.53 us -> none  [from_everyone(): copies = jnp.broadcast_to(value, (lax.axis_size(axis), *value.shape))]
    squeeze x4 -> x0, local copies, waits for them, and re-layouts: 4.23 us -> none  [the longest x1 3.33 us: per_device(): spec_layer = spectral[layer]]
  transfers between devices with their start and end apart: 11 -> 0, of which waited for: 8 -> 0; matrix products, arithmetic and copies ran while one was open for 3% -> 0% of each run, Pallas kernels for 0% -> 0%
where the time goes in v2:
time: 100 us; the launch traced here: 99.9 us
  Pallas kernels  98.1 us (98%)
  local copies, waits for them, and re-layouts  1.77 us (2%)
    pallas_call x1, Pallas kernels, per_device(): pl.pallas_call(kernel, out_shape=jax.ShapeDtypeStruct(tokens.shape, F32),...  98.1 us

profile of v2, /device:TPU:1, one launch (start us, length us, event | category | flops | bytes accessed | tf_op | source)
XLA Modules:
  0.0 99.9 jit_solution(6074644137983560859)
XLA Ops:
  0.0 98.1 %blocks.1 = f32[2,96,512]{2,1,0:T(8,128)} custom-call(f32[2,96,512]{2,1,0:T(8,128)} %refs_0_.1, f32[2,64,96,128]{3,2,1,0:T(8,128)} %refs_1_.1, f32[2,96]{1,0:T(2,128)} %refs_2_.1, f32[2,96]{1,0:T(2,128)} %refs_3_.1, bf16[2,3,8,384]{3,2,1,0:T(8,128)(2,1)} %bitcast.4, bf16[2,384]{1,0:T(2,128)(2,1)} %refs_5_.1, bf16[2,3,8,384]{3,2,1,0:T(8,128)(2,1)} %bitcast.5, ...), custom_call_target="tpu_custom_call" | custom-call | tf_op jit(solution)/shard_map/blocks/pallas_call | solution.py:488
  98.1 1.8 %copy.15 = f32[2,96,512]{2,1,0:T(8,128)} copy(f32[2,96,512]{2,1,0:T(8,128)} %blocks.1) | data formatting | bytes 786432

commit v3 on v2

--- a/solution.py
+++ b/solution.py
@@ -74,10 +74,10 @@
         (there_tx, there_rx, back_tx, back_rx, ag_tx, ag_rx, rs_tx, rs_rx),
         (w_all, et, st, gcol, bcol, turn),
         (in_sem, spec_sem, small_s, small_r, stats_s, stats_r, there_s, there_r, back_s, back_r),
-        (ag_s, ag_r, rs_s, rs_r, wy_s, wy_r, wz_s, wz_r, wc_s, wc_r),
+        (ag_s, ag_r, rs_s, rs_r, wy_s, wy_r, wz_s, wz_r, wc_s, wc_r, near_sem, far_sem),
     ) = [
         tuple(refs[a:b])
-        for a, b in zip((0, 7, 13, 14, 20, 27, 35, 41, 51), (7, 13, 14, 20, 27, 35, 41, 51, 61))
+        for a, b in zip((0, 7, 13, 14, 20, 27, 35, 41, 51), (7, 13, 14, 20, 27, 35, 41, 51, 63))
     ]
     fwd_rows, fwd_lanes, inv_lanes, inv_rows, spread, gather = table
 
@@ -98,9 +98,15 @@
 
     barrier = pltpu.get_barrier_semaphore()
 
-    def greet_row(t, carry):
-        pl.semaphore_signal(barrier, inc=1, device_id=((r + t) % NR, c), device_id_type=MESH)
-        return carry
+    def greet_rows(sem, shifts_z, shifts_y=()):
+        for t in shifts_z:
+            pl.semaphore_signal(
+                sem, inc=1, device_id=((z + NZ + t) % NZ * NY + y, c), device_id_type=MESH
+            )
+        for t in shifts_y:
+            pl.semaphore_signal(
+                sem, inc=1, device_id=(z * NY + (y + t) % NY, c), device_id_type=MESH
+            )
 
     def greet_chan(t, carry):
         pl.semaphore_signal(barrier, inc=1, device_id=(r, (c + t) % NC), device_id_type=MESH)
@@ -162,19 +168,29 @@
 
     def enter():
         lax.fori_loop(1, NC, greet_chan, 0)
-        lax.fori_loop(1, NR, greet_row, 0)
+        greet_rows(barrier, (-2, -1, 1, 2), (1, 2, 3))
         for copy in loads:
             copy.start()
         for layer in range(LAYERS):
             for i in range(OWN):
                 spec_copy(layer, i).start()
+                pending["spec", layer, i] = spec_copy(layer, i).wait
         small_rx[c] = jnp.zeros((4, PIX), F32)
         turn[...] = jnp.zeros((128, 128), F32)
         for copy in loads:
             copy.wait()
         small_rx[c, 0:2, 0:CH] = gm_buf[...]
         small_rx[c, 2:4, 0:HID] = b_buf[...].astype(F32)
-        pl.semaphore_wait(barrier, NR - 1 + NC - 1)
+        pl.semaphore_wait(barrier, NC - 1 + 7)
+        greet_rows(near_sem, (-2, -1, 1, 2))
+
+
+    def hear_near():
+        pl.semaphore_wait(near_sem, 4)
+        greet_rows(far_sem, (-2, 2))
+
+    def hear_far():
+        pl.semaphore_wait(far_sem, 2)
 
     def send_small():
         to_all("small", lambda to: small_rx.at[c], small_rx, small_s, small_r, False)
@@ -183,7 +199,7 @@
         lanes = lax.broadcasted_iota(jnp.int32, (1, CH), 1)
         for layer in range(LAYERS):
             for i in range(OWN):
-                spec_copy(layer, i).wait()
+                owed(("spec", layer, i))
                 values = spec_buf.at[layer, i].reshape(GRID * 8, 128)[pl.ds(r % 8, GRID, stride=8), :]
                 gain = jnp.sum(
                     jnp.where(lanes == i * NR + r, gi_buf[layer : layer + 1, :], 0.0),
@@ -414,18 +430,20 @@
             then(name, f, layer, s)
 
     each("stats", send_stats, 0)
+    then("near", hear_near)
     then("wy", wy, 0)
     then("small", send_small)
+    then("wy", wy, 1)
     then("filters", filters)
+    then("far", hear_far)
     then("wz", wz, 0, 1)
     each("there", there, 0)
     then("columns", columns)
+    then("wz", wz, 0, 2)
     each("transform", transform, 0)
-    then("wz", wz, 0, 2)
-    then("wy", wy, 1)
-    each("share", share, 0)
     then("wz", wz, 0, 3)
     then("wz", wz, 0, 4)
+    each("share", share, 0)
     then("wc", wc, 0)
     then("wz", wz, 1, 1)
     then("weights", weights, 0)
@@ -485,9 +503,10 @@
     ]
     scratch += [dma((LAYERS, NS))] * 10
     scratch += [dma((LAYERS, NY))] * 2 + [dma((LAYERS, 4, 2))] * 2 + [dma((LAYERS,))] * 2
+    scratch += [pltpu.SemaphoreType.REGULAR] * 2
     return pl.pallas_call(
         kernel,
-        out_shape=jax.ShapeDtypeStruct(tokens.shape, F32),
+        out_shape=pltpu.VMEM(tokens.shape, F32),
         in_specs=[hbm] * 13,
         out_specs=pl.BlockSpec(memory_space=pltpu.VMEM),
         scratch_shapes=scratch,

time: 100 us -> 96 us (0.960)
  Pallas kernels: 98.1 us -> 95.1 us
  local copies, waits for them, and re-layouts: 1.77 us -> 0.75 us
    pallas_call x1, Pallas kernels: 98.1 us -> 95.1 us  [per_device(): pl.pallas_call(kernel, out_shape=pltpu.VMEM(tokens.shape, F32), in_specs=...]
    unnamed x1, local copies, waits for them, and re-layouts: 1.77 us -> 0.75 us
where the time goes in v3:
time: 96 us; the launch traced here: 95.9 us
  Pallas kernels  95.1 us (99%)
    pallas_call x1, Pallas kernels, per_device(): pl.pallas_call(kernel, out_shape=pltpu.VMEM(tokens.shape, F32), in_specs=...  95.1 us

profile of v3, /device:TPU:1, one launch (start us, length us, event | category | flops | bytes accessed | tf_op | source)
XLA Modules:
  0.0 95.9 jit_solution(8784938291205011193)
XLA Ops:
  0.0 95.1 %blocks.1 = f32[2,96,512]{2,1,0:T(8,128)S(1)} custom-call(f32[2,96,512]{2,1,0:T(8,128)} %refs_0_.1, f32[2,64,96,128]{3,2,1,0:T(8,128)} %refs_1_.1, f32[2,96]{1,0:T(2,128)} %refs_2_.1, f32[2,96]{1,0:T(2,128)} %refs_3_.1, bf16[2,3,8,384]{3,2,1,0:T(8,128)(2,1)} %bitcast.4, bf16[2,384]{1,0:T(2,128)(2,1)} %refs_5_.1, bf16[2,3,8,384]{3,2,1,0:T(8,128)(2,1)} %bitcast.5, ...), custom_call_target="tpu_custom_call" | custom-call | tf_op jit(solution)/shard_map/blocks/pallas_call | solution.py:507
  95.1 0.7 copy.15

commit v4 on v3

--- a/solution.py
+++ b/solution.py
@@ -71,13 +71,13 @@
         (out,),
         table,
         (gi_buf, gm_buf, b_buf, spec_buf, filt, small_rx, stats_rx),
-        (there_tx, there_rx, back_tx, back_rx, ag_tx, ag_rx, rs_tx, rs_rx),
+        (there_tx, there_rx, back_tx, back_rx, ag_tx, ag_rx, rs_tx, rs_rx, rl_tx, rl_rx),
         (w_all, et, st, gcol, bcol, turn),
         (in_sem, spec_sem, small_s, small_r, stats_s, stats_r, there_s, there_r, back_s, back_r),
         (ag_s, ag_r, rs_s, rs_r, wy_s, wy_r, wz_s, wz_r, wc_s, wc_r, near_sem, far_sem),
     ) = [
         tuple(refs[a:b])
-        for a, b in zip((0, 7, 13, 14, 20, 27, 35, 41, 51), (7, 13, 14, 20, 27, 35, 41, 51, 63))
+        for a, b in zip((0, 7, 13, 14, 20, 27, 37, 43, 53), (7, 13, 14, 20, 27, 37, 43, 53, 65))
     ]
     fwd_rows, fwd_lanes, inv_lanes, inv_rows, spread, gather = table
 
@@ -85,6 +85,8 @@
     c = lax.axis_index("chan")
     z, y = r // NY, r % NY
     x, core = c // 2, c % 2
+    above, below, across = (x + 1) % 4, (x + 3) % 4, (x + 2) % 4
+    halves = (pl.ds(0, CH // 2), pl.ds(CH // 2, CH // 2))
 
     pending = {}
     leaving = []
@@ -94,6 +96,11 @@
 
     def wait(*key):
         return lambda: owed(key)
+
+    def remote(src, dst, send, recv, to):
+        pltpu.make_async_remote_copy(
+            src_ref=src, dst_ref=dst, send_sem=send, recv_sem=recv, device_id=(r, to), device_id_type=MESH
+        ).start()
 
 
     barrier = pltpu.get_barrier_semaphore()
@@ -138,11 +145,11 @@
             stats_rx[layer, s, c, hl : hl + 1, :] = jnp.sum(value, axis=0, keepdims=True)
             stats_rx[layer, s, c, hl + 2 : hl + 3, :] = jnp.sum(value * value, axis=0, keepdims=True)
 
-    def to_all(key, source, target, send, recv, whole):
+    def to_all(key, target, send, recv):
         def one(t, carry):
             to = (c + t) % NC
             pltpu.make_async_remote_copy(
-                src_ref=source(to),
+                src_ref=target.at[c],
                 dst_ref=target.at[c],
                 send_sem=send,
                 recv_sem=recv,
@@ -152,19 +159,13 @@
             return carry
 
         lax.fori_loop(1, NC, one, 0)
-        if whole:
-            pltpu.make_async_copy(source(c), target.at[c], recv).start()
-            pending[key] = lambda: arrived(target, recv)
-        else:
-            pending[key] = lambda: arrived(target.at[pl.ds(0, NC - 1)], recv)
+        pending[key] = lambda: arrived(target.at[pl.ds(0, NC - 1)], recv)
         leaving.append(lambda: arrived(target.at[pl.ds(0, NC - 1)], send))
 
     def send_stats(layer, s):
         put_stats(layer, s)
         buf = stats_rx.at[layer, s]
-        to_all(
-            ("stats", layer, s), lambda to: buf.at[c], buf, stats_s.at[layer, s], stats_r.at[layer, s], False
-        )
+        to_all(("stats", layer, s), buf, stats_s.at[layer, s], stats_r.at[layer, s])
 
     def enter():
         lax.fori_loop(1, NC, greet_chan, 0)
@@ -193,7 +194,7 @@
         pl.semaphore_wait(far_sem, 2)
 
     def send_small():
-        to_all("small", lambda to: small_rx.at[c], small_rx, small_s, small_r, False)
+        to_all("small", small_rx, small_s, small_r)
 
     def filters():
         lanes = lax.broadcasted_iota(jnp.int32, (1, CH), 1)
@@ -380,17 +381,40 @@
                     ag_tx[layer, s, hl, i * NR : (i + 1) * NR, pair * 128 : (pair + 1) * 128] = mixed[
                         row : row + NR, i * 128 : (i + 1) * 128
                     ]
-        to_all(
-            ("ag", layer, s),
-            lambda to: ag_tx.at[layer, s, to % 2],
-            ag_rx.at[layer, s],
-            ag_s.at[layer, s],
-            ag_r.at[layer, s],
-            True,
-        )
+        own = ag_rx.at[layer, s, c]
+        send, recv = ag_s.at[layer, s, 0], ag_r.at[layer, s]
+        for way, chip in enumerate((above, below)):
+            for k in range(2):
+                remote(ag_tx.at[layer, s, k], own, send, recv.at[1 + way], 2 * chip + k)
+        remote(ag_tx.at[layer, s, 1 - core], own, send, recv.at[0], 2 * x + 1 - core)
+        pltpu.make_async_copy(ag_tx.at[layer, s, core], own, recv.at[0]).start()
+        two = ag_rx.at[layer, s, pl.ds(0, 2)]
+
+        def near():
+            arrived(two, recv.at[1])
+            arrived(two, recv.at[2])
+
+        pending["ag", layer, s] = lambda: arrived(two, recv.at[0])
+        pending["near", layer, s] = near
+        leaving.append(lambda: arrived(ag_rx.at[layer, s, pl.ds(0, 5)], send))
+
+    def forward(layer, s):
+        owed(("near", layer, s))
+        send, recv = ag_s.at[layer, s, 1], ag_r.at[layer, s]
+        for way, (origin, chip) in enumerate(((below, above), (above, below))):
+            ref = ag_rx.at[layer, s, pl.ds(2 * origin, 2), halves[way]]
+            remote(ref, ref, send, recv.at[3 + way], 2 * chip + core)
+
+        def further():
+            for way in range(2):
+                arrived(ag_rx.at[layer, s, pl.ds(2 * across, 2), halves[way]], recv.at[3 + way])
+
+        pending["far", layer, s] = further
+        leaving.append(lambda: arrived(ag_rx.at[layer, s, pl.ds(0, 2)], send))
 
     def mlp(layer, s):
         owed(("ag", layer, s))
+        owed(("far", layer, s))
         value = ag_rx[layer, s].astype(F32).reshape(768, WIDE)
         mean = jnp.sum(value, axis=0, keepdims=True) * (1.0 / 768.0)
         square = jnp.sum(value * value, axis=0, keepdims=True) * (1.0 / 768.0)
@@ -399,22 +423,60 @@
         hidden = jax.nn.gelu(dot(et[layer], normed2) + bcol[layer], approximate=True)
         part = dot(st[layer], hidden.astype(BF16))
         rs_tx[layer, s] = part.astype(BF16).reshape(NC, CH, WIDE)
-        to_all(
-            ("rs", layer, s),
-            lambda to: rs_tx.at[layer, s, to],
-            rs_rx.at[layer, s],
-            rs_s.at[layer, s],
-            rs_r.at[layer, s],
-            True,
-        )
+        tx, rx = rs_tx.at[layer, s], rs_rx.at[layer, s]
+        send, recv = rs_s.at[layer, s, 0], rs_r.at[layer, s]
+        for way, chip in enumerate((above, below)):
+            ref = tx.at[pl.ds(2 * across, 2), halves[way]]
+            remote(ref, rl_rx.at[layer, s, way], send, recv.at[3 + way], 2 * chip + core)
+        for way, chip in enumerate((above, below)):
+            for k in range(2):
+                remote(
+                    tx.at[2 * chip + k, halves[1 - way]],
+                    rx.at[1 + way, core, halves[1 - way]],
+                    send,
+                    recv.at[1 + way],
+                    2 * chip + k,
+                )
+        remote(tx.at[2 * x + 1 - core], rx.at[0, core], send, recv.at[0], 2 * x + 1 - core)
+        pltpu.make_async_copy(tx.at[c], rx.at[0, core], recv.at[0]).start()
+
+        def parts():
+            for way in range(2):
+                arrived(rl_rx.at[layer, s, way], recv.at[3 + way])
+
+        def sums():
+            for slot in range(3):
+                arrived(rx.at[slot], recv.at[slot])
+
+        pending["rl", layer, s] = parts
+        pending["rs", layer, s] = sums
+        leaving.append(lambda: arrived(ag_rx.at[layer, s, pl.ds(0, 5)], send))
+
+    def relay(layer, s):
+        owed(("rl", layer, s))
+        send, recv = rs_s.at[layer, s, 1], rs_r.at[layer, s]
+        for way, chip in enumerate((above, below)):
+            for k in range(2):
+                both = rl_rx[layer, s, way, k].astype(F32) + rs_tx[
+                    layer, s, 2 * chip + k, halves[way]
+                ].astype(F32)
+                rl_tx[layer, s, way, k] = both.astype(BF16)
+                remote(
+                    rl_tx.at[layer, s, way, k],
+                    rs_rx.at[layer, s, 1 + way, core, halves[way]],
+                    send,
+                    recv.at[1 + way],
+                    2 * chip + k,
+                )
+        leaving.append(lambda: arrived(ag_rx.at[layer, s, pl.ds(0, 2)], send))
 
     def add(layer, s):
         owed(("rs", layer, s))
         at = slice(s * WIDE, (s + 1) * WIDE)
         for hl in range(2):
-            total = rs_rx[layer, s, hl].astype(F32)
-            for chip in range(1, 4):
-                total = total + rs_rx[layer, s, 2 * chip + hl].astype(F32)
+            total = rs_rx[layer, s, 0, hl].astype(F32)
+            for slot in range(1, 3):
+                total = total + rs_rx[layer, s, slot, hl].astype(F32)
             out[hl, :, at] = out[hl, :, at] + total.astype(BF16).astype(F32)
         if layer + 1 < LAYERS:
             send_stats(layer + 1, s)
@@ -434,10 +496,10 @@
     then("wy", wy, 0)
     then("small", send_small)
     then("wy", wy, 1)
-    then("filters", filters)
     then("far", hear_far)
     then("wz", wz, 0, 1)
     each("there", there, 0)
+    then("filters", filters)
     then("columns", columns)
     then("wz", wz, 0, 2)
     each("transform", transform, 0)
@@ -446,8 +508,10 @@
     each("share", share, 0)
     then("wc", wc, 0)
     then("wz", wz, 1, 1)
+    each("forward", forward, 0)
     then("weights", weights, 0)
     each("mlp", mlp, 0)
+    each("relay", relay, 0)
     then("wz", wz, 1, 2)
     then("wz", wz, 1, 3)
     each("add", add, 0)
@@ -457,7 +521,9 @@
     each("transform", transform, 1)
     then("weights", weights, 1)
     each("share", share, 1)
+    each("forward", forward, 1)
     each("mlp", mlp, 1)
+    each("relay", relay, 1)
     each("add", add, 1)
 
     for _, step in plan[:STOP]:
@@ -489,7 +555,9 @@
         pltpu.VMEM((LAYERS, NS, 2, CH, WIDE), BF16),
         pltpu.VMEM((LAYERS, NS, NC, CH, WIDE), BF16),
         pltpu.VMEM((LAYERS, NS, NC, CH, WIDE), BF16),
-        pltpu.VMEM((LAYERS, NS, NC, CH, WIDE), BF16),
+        pltpu.VMEM((LAYERS, NS, 3, 2, CH, WIDE), BF16),
+        pltpu.VMEM((LAYERS, NS, 2, 2, CH // 2, WIDE), BF16),
+        pltpu.VMEM((LAYERS, NS, 2, 2, CH // 2, WIDE), BF16),
         pltpu.VMEM((LAYERS, 2, NZ, NY, 6, 8, HID), BF16),
         pltpu.VMEM((LAYERS, 768, 768), BF16),
         pltpu.VMEM((LAYERS, 768, 768), BF16),
@@ -501,7 +569,8 @@
         dma(()),
         dma(()),
     ]
-    scratch += [dma((LAYERS, NS))] * 10
+    scratch += [dma((LAYERS, NS))] * 6
+    scratch += [dma((LAYERS, NS, 2)), dma((LAYERS, NS, 5))] * 2
     scratch += [dma((LAYERS, NY))] * 2 + [dma((LAYERS, 4, 2))] * 2 + [dma((LAYERS,))] * 2
     scratch += [pltpu.SemaphoreType.REGULAR] * 2
     return pl.pallas_call(

time: 96 us -> 99.9 us (1.041)
  Pallas kernels: 95.1 us -> 99 us
    pallas_call x1, Pallas kernels: 95.1 us -> 99 us  [per_device(): pl.pallas_call(kernel, out_shape=pltpu.VMEM(tokens.shape, F32), in_specs=...]
where the time goes in v4:
time: 99.9 us; the launch traced here: 99.8 us
  Pallas kernels  99 us (99%)
    pallas_call x1, Pallas kernels, per_device(): pl.pallas_call(kernel, out_shape=pltpu.VMEM(tokens.shape, F32), in_specs=...  99 us

profile of v4, /device:TPU:1, one launch (start us, length us, event | category | flops | bytes accessed | tf_op | source)
XLA Modules:
  0.0 99.8 jit_solution(9308041950469440099)
XLA Ops:
  0.0 99.0 %blocks.1 = f32[2,96,512]{2,1,0:T(8,128)S(1)} custom-call(f32[2,96,512]{2,1,0:T(8,128)} %refs_0_.1, f32[2,64,96,128]{3,2,1,0:T(8,128)} %refs_1_.1, f32[2,96]{1,0:T(2,128)} %refs_2_.1, f32[2,96]{1,0:T(2,128)} %refs_3_.1, bf16[2,3,8,384]{3,2,1,0:T(8,128)(2,1)} %bitcast.4, bf16[2,384]{1,0:T(2,128)(2,1)} %refs_5_.1, bf16[2,3,8,384]{3,2,1,0:T(8,128)(2,1)} %bitcast.5, ...), custom_call_target="tpu_custom_call" | custom-call | tf_op jit(solution)/shard_map/blocks/pallas_call | solution.py:576
  99.0 0.7 copy.15

commit v5 on v4

--- a/solution.py
+++ b/solution.py
@@ -93,9 +93,6 @@
 
     def owed(key):
         pending.pop(key)()
-
-    def wait(*key):
-        return lambda: owed(key)
 
     def remote(src, dst, send, recv, to):
         pltpu.make_async_remote_copy(
@@ -295,8 +292,7 @@
 
 
     def exchange(key, tx, rx, send, recv):
-        def one(t, carry):
-            to = (r + t) % NR
+        def send_to(to):
             pltpu.make_async_remote_copy(
                 src_ref=tx.at[to],
                 dst_ref=rx.at[r],
@@ -305,9 +301,15 @@
                 device_id=(to, c),
                 device_id_type=MESH,
             ).start()
+
+        def one(t, carry):
+            step = (t // NY + 1) // 2 * (t // NY % 2 * 2 - 1)
+            send_to((z + NZ // 2 + step + NZ) % NZ * NY + (y + 2 + t) % NY)
             return carry
 
-        lax.fori_loop(1, NR, one, 0)
+        lax.fori_loop(0, NR - NY, one, 0)
+        for t in range(1, NY):
+            send_to(z * NY + (y + t) % NY)
         pltpu.make_async_copy(tx.at[r], rx.at[r], recv).start()
         pending[key] = lambda: arrived(rx, recv)
         leaving.append(lambda: arrived(tx.at[pl.ds(0, NR - 1)], send))
@@ -382,7 +384,9 @@
                         row : row + NR, i * 128 : (i + 1) * 128
                     ]
         own = ag_rx.at[layer, s, c]
-        send, recv = ag_s.at[layer, s, 0], ag_r.at[layer, s]
+        send, recv = ag_s.at[layer, s], ag_r.at[layer, s]
+        for k in range(2):
+            remote(ag_tx.at[layer, s, k], own, send, recv.at[3], 2 * across + k)
         for way, chip in enumerate((above, below)):
             for k in range(2):
                 remote(ag_tx.at[layer, s, k], own, send, recv.at[1 + way], 2 * chip + k)
@@ -390,31 +394,15 @@
         pltpu.make_async_copy(ag_tx.at[layer, s, core], own, recv.at[0]).start()
         two = ag_rx.at[layer, s, pl.ds(0, 2)]
 
-        def near():
-            arrived(two, recv.at[1])
-            arrived(two, recv.at[2])
-
-        pending["ag", layer, s] = lambda: arrived(two, recv.at[0])
-        pending["near", layer, s] = near
-        leaving.append(lambda: arrived(ag_rx.at[layer, s, pl.ds(0, 5)], send))
-
-    def forward(layer, s):
-        owed(("near", layer, s))
-        send, recv = ag_s.at[layer, s, 1], ag_r.at[layer, s]
-        for way, (origin, chip) in enumerate(((below, above), (above, below))):
-            ref = ag_rx.at[layer, s, pl.ds(2 * origin, 2), halves[way]]
-            remote(ref, ref, send, recv.at[3 + way], 2 * chip + core)
-
-        def further():
-            for way in range(2):
-                arrived(ag_rx.at[layer, s, pl.ds(2 * across, 2), halves[way]], recv.at[3 + way])
-
-        pending["far", layer, s] = further
-        leaving.append(lambda: arrived(ag_rx.at[layer, s, pl.ds(0, 2)], send))
+        def blocks():
+            for k in range(4):
+                arrived(two, recv.at[k])
+
+        pending["ag", layer, s] = blocks
+        leaving.append(lambda: arrived(ag_rx.at[layer, s, pl.ds(0, 7)], send))
 
     def mlp(layer, s):
         owed(("ag", layer, s))
-        owed(("far", layer, s))
         value = ag_rx[layer, s].astype(F32).reshape(768, WIDE)
         mean = jnp.sum(value, axis=0, keepdims=True) * (1.0 / 768.0)
         square = jnp.sum(value * value, axis=0, keepdims=True) * (1.0 / 768.0)
@@ -491,37 +479,35 @@
         for s in range(NS):
             then(name, f, layer, s)
 
+    then("wy", wy, 0)
     each("stats", send_stats, 0)
     then("near", hear_near)
-    then("wy", wy, 0)
+    then("wz", wz, 0, 1)
     then("small", send_small)
     then("wy", wy, 1)
     then("far", hear_far)
-    then("wz", wz, 0, 1)
     each("there", there, 0)
+    then("wz", wz, 0, 2)
     then("filters", filters)
     then("columns", columns)
-    then("wz", wz, 0, 2)
     each("transform", transform, 0)
     then("wz", wz, 0, 3)
+    each("share", share, 0)
     then("wz", wz, 0, 4)
-    each("share", share, 0)
     then("wc", wc, 0)
     then("wz", wz, 1, 1)
-    each("forward", forward, 0)
     then("weights", weights, 0)
+    then("wz", wz, 1, 2)
     each("mlp", mlp, 0)
     each("relay", relay, 0)
-    then("wz", wz, 1, 2)
     then("wz", wz, 1, 3)
     each("add", add, 0)
+    each("there", there, 1)
     then("wz", wz, 1, 4)
-    each("there", there, 1)
+    each("transform", transform, 1)
     then("wc", wc, 1)
-    each("transform", transform, 1)
+    each("share", share, 1)
     then("weights", weights, 1)
-    each("share", share, 1)
-    each("forward", forward, 1)
     each("mlp", mlp, 1)
     each("relay", relay, 1)
     each("add", add, 1)
@@ -570,7 +556,8 @@
         dma(()),
     ]
     scratch += [dma((LAYERS, NS))] * 6
-    scratch += [dma((LAYERS, NS, 2)), dma((LAYERS, NS, 5))] * 2
+    scratch += [dma((LAYERS, NS)), dma((LAYERS, NS, 4))]
+    scratch += [dma((LAYERS, NS, 2)), dma((LAYERS, NS, 5))]
     scratch += [dma((LAYERS, NY))] * 2 + [dma((LAYERS, 4, 2))] * 2 + [dma((LAYERS,))] * 2
     scratch += [pltpu.SemaphoreType.REGULAR] * 2
     return pl.pallas_call(

time: 99.9 us -> 89.2 us (0.89)
  Pallas kernels: 99 us -> 88.3 us
    pallas_call x1, Pallas kernels: 99 us -> 88.3 us  [per_device(): pl.pallas_call(kernel, out_shape=pltpu.VMEM(tokens.shape, F32), in_specs=...]
where the time goes in v5:
time: 89.2 us; the launch traced here: 89.1 us
  Pallas kernels  88.3 us (99%)
    pallas_call x1, Pallas kernels, per_device(): pl.pallas_call(kernel, out_shape=pltpu.VMEM(tokens.shape, F32), in_specs=...  88.3 us

profile of v5, /device:TPU:1, one launch (start us, length us, event | category | flops | bytes accessed | tf_op | source)
XLA Modules:
  0.0 89.1 jit_solution(7201111211109240774)
XLA Ops:
  0.0 88.3 %blocks.1 = f32[2,96,512]{2,1,0:T(8,128)S(1)} custom-call(f32[2,96,512]{2,1,0:T(8,128)} %refs_0_.1, f32[2,64,96,128]{3,2,1,0:T(8,128)} %refs_1_.1, f32[2,96]{1,0:T(2,128)} %refs_2_.1, f32[2,96]{1,0:T(2,128)} %refs_3_.1, bf16[2,3,8,384]{3,2,1,0:T(8,128)(2,1)} %bitcast.4, bf16[2,384]{1,0:T(2,128)(2,1)} %refs_5_.1, bf16[2,3,8,384]{3,2,1,0:T(8,128)(2,1)} %bitcast.5, ...), custom_call_target="tpu_custom_call" | custom-call | tf_op jit(solution)/shard_map/blocks/pallas_call | solution.py:563
  88.3 0.7 copy.15

commit v6 on v5

--- a/solution.py
+++ b/solution.py
@@ -71,13 +71,13 @@
         (out,),
         table,
         (gi_buf, gm_buf, b_buf, spec_buf, filt, small_rx, stats_rx),
-        (there_tx, there_rx, back_tx, back_rx, ag_tx, ag_rx, rs_tx, rs_rx, rl_tx, rl_rx),
+        (there_tx, there_rx, back_tx, back_rx, ag_tx, ag_rx, rs_tx, rs_rx),
         (w_all, et, st, gcol, bcol, turn),
         (in_sem, spec_sem, small_s, small_r, stats_s, stats_r, there_s, there_r, back_s, back_r),
-        (ag_s, ag_r, rs_s, rs_r, wy_s, wy_r, wz_s, wz_r, wc_s, wc_r, near_sem, far_sem),
+        (ag_s, ag_r, rs_s, rs_r, wy_s, wy_r, wz_s, wz_r, wc_s, wc_r, near_sem, far_sem, wd_r),
     ) = [
         tuple(refs[a:b])
-        for a, b in zip((0, 7, 13, 14, 20, 27, 37, 43, 53), (7, 13, 14, 20, 27, 37, 43, 53, 65))
+        for a, b in zip((0, 7, 13, 14, 20, 27, 35, 41, 51), (7, 13, 14, 20, 27, 35, 41, 51, 64))
     ]
     fwd_rows, fwd_lanes, inv_lanes, inv_rows, spread, gather = table
 
@@ -86,7 +86,6 @@
     z, y = r // NY, r % NY
     x, core = c // 2, c % 2
     above, below, across = (x + 1) % 4, (x + 3) % 4, (x + 2) % 4
-    halves = (pl.ds(0, CH // 2), pl.ds(CH // 2, CH // 2))
 
     pending = {}
     leaving = []
@@ -252,14 +251,29 @@
                 w_all.at[layer, core, z, (y + NY - t) % NY],
             )
 
+    def to_core(layer, parts, last=False):
+        for ref in parts:
+            pltpu.make_async_remote_copy(
+                src_ref=ref,
+                dst_ref=ref,
+                send_sem=wc_s.at[layer],
+                recv_sem=wc_r.at[layer],
+                device_id=(r, x * 2 + 1 - core),
+                device_id_type=MESH,
+            ).start()
+        if last:
+            pending["w", layer] = lambda: arrived(w_all.at[layer, 1 - core], wc_r.at[layer])
+            leaving.append(lambda: arrived(w_all.at[layer, core], wc_s.at[layer]))
+
     def wz_ref(layer, step, way, shift):
         at = (z + 2 * NZ - shift) % NZ if way == 0 else (z + shift) % NZ
         ref = w_all.at[layer, core, at]
         return ref.at[pl.ds(2 * way, 2)] if step == 4 else ref
 
     def wz(layer, step):
-        if ("w", layer, step - 1) in pending:
-            owed(("w", layer, step - 1))
+        owed(("w", layer, step - 1))
+        came = (0, 1) if step > 1 else (0,)
+        to_core(layer, [wz_ref(layer, 0, way, step - 1) for way in came])
         for way in range(2):
             to = (z + 1) % NZ if way == 0 else (z + NZ - 1) % NZ
             move(
@@ -273,17 +287,75 @@
 
     def wc(layer):
         owed(("w", layer, 4))
-        move(
-            w_all.at[layer, core],
-            wc_s.at[layer],
-            wc_r.at[layer],
-            (r, x * 2 + 1 - core),
-            ("w", layer, 5),
-            w_all.at[layer, 1 - core],
-        )
+        to_core(layer, [wz_ref(layer, 0, 0, 4)], last=True)
+
+
+    near_z, far_z = (0, 1, 2, 6, 7), (3, 4, 5)
+    on_way = (((0, 1, 2), (6, 7)), ((3,), (4, 5)))
+
+    def shard(dz, dy):
+        return w_all.at[0, core, (z + dz) % NZ, (y + NY + dy) % NY]
+
+    def shards(count):
+        return w_all.at[0, core, pl.ds(0, count), 0]
+
+    def wd():
+        own = shard(0, 0)
+        for t in (1, 7, 2, 6, 3, 5, 4):
+            pltpu.make_async_remote_copy(
+                src_ref=own,
+                dst_ref=own,
+                send_sem=wy_s.at[0, 0],
+                recv_sem=wd_r.at[NZ - t],
+                device_id=((z + t) % NZ * NY + y, c),
+                device_id_type=MESH,
+            ).start()
+            pending["wd", t] = lambda t=t: arrived(shard(t, 0), wd_r.at[t])
+        leaving.append(lambda: arrived(shards(NZ - 1), wy_s.at[0, 0]))
+        leaving.append(lambda: arrived(w_all.at[0, core, pl.ds(0, 6)], wz_s.at[0, 0, 0]))
+
+    def round_y(ref, way, sem):
+        to = (y + 1) % NY if way == 0 else (y + NY - 1) % NY
+        pltpu.make_async_remote_copy(
+            src_ref=ref,
+            dst_ref=ref,
+            send_sem=wz_s.at[0, 0, 0],
+            recv_sem=sem,
+            device_id=(z * NY + to, c),
+            device_id_type=MESH,
+        ).start()
+
+    def wr(group):
+        members = (near_z, far_z)[group]
+        for dz in members:
+            if dz:
+                owed(("wd", dz))
+        for way in range(2):
+            sem = wz_r.at[0, group, way]
+            for dz in members:
+                round_y(shard(dz, 0), way, sem)
+            pending["wr", group, way] = lambda sem=sem: arrived(shards(len(members)), sem)
+        to_core(0, [shard(dz, 0) for dz in members])
+
+    def ws(group):
+        members = (near_z, far_z)[group]
+        for way in range(2):
+            owed(("wr", group, way))
+        for way in range(2):
+            sem = wz_r.at[0, 2 + group, way]
+            chosen = on_way[group][way]
+            for dz in chosen:
+                round_y(shard(dz, (-1, 1)[way]), way, sem)
+            pending["ws", group, way] = lambda sem=sem, n=len(chosen): arrived(shards(n), sem)
+        to_core(0, [shard(dz, dy) for dz in members for dy in (-1, 1)])
+
+    def we(group):
+        for way in range(2):
+            owed(("ws", group, way))
+        to_core(0, [shard(dz, 2) for dz in (near_z, far_z)[group]], last=group == 1)
 
     def weights(layer):
-        owed(("w", layer, 5))
+        owed(("w", layer))
         for k in range(2):
             e = w_all[layer, k, :, :, 0:3].astype(F32).reshape(768, HID)
             et[layer, k * HID : (k + 1) * HID, :] = e.T.astype(BF16)
@@ -412,58 +484,26 @@
         part = dot(st[layer], hidden.astype(BF16))
         rs_tx[layer, s] = part.astype(BF16).reshape(NC, CH, WIDE)
         tx, rx = rs_tx.at[layer, s], rs_rx.at[layer, s]
-        send, recv = rs_s.at[layer, s, 0], rs_r.at[layer, s]
-        for way, chip in enumerate((above, below)):
-            ref = tx.at[pl.ds(2 * across, 2), halves[way]]
-            remote(ref, rl_rx.at[layer, s, way], send, recv.at[3 + way], 2 * chip + core)
-        for way, chip in enumerate((above, below)):
+        send, recv = rs_s.at[layer, s], rs_r.at[layer, s]
+        for slot, chip in ((3, across), (1, above), (2, below)):
             for k in range(2):
-                remote(
-                    tx.at[2 * chip + k, halves[1 - way]],
-                    rx.at[1 + way, core, halves[1 - way]],
-                    send,
-                    recv.at[1 + way],
-                    2 * chip + k,
-                )
+                remote(tx.at[2 * chip + k], rx.at[slot, core], send, recv.at[slot], 2 * chip + k)
         remote(tx.at[2 * x + 1 - core], rx.at[0, core], send, recv.at[0], 2 * x + 1 - core)
         pltpu.make_async_copy(tx.at[c], rx.at[0, core], recv.at[0]).start()
 
-        def parts():
-            for way in range(2):
-                arrived(rl_rx.at[layer, s, way], recv.at[3 + way])
-
         def sums():
-            for slot in range(3):
+            for slot in range(4):
                 arrived(rx.at[slot], recv.at[slot])
 
-        pending["rl", layer, s] = parts
         pending["rs", layer, s] = sums
-        leaving.append(lambda: arrived(ag_rx.at[layer, s, pl.ds(0, 5)], send))
-
-    def relay(layer, s):
-        owed(("rl", layer, s))
-        send, recv = rs_s.at[layer, s, 1], rs_r.at[layer, s]
-        for way, chip in enumerate((above, below)):
-            for k in range(2):
-                both = rl_rx[layer, s, way, k].astype(F32) + rs_tx[
-                    layer, s, 2 * chip + k, halves[way]
-                ].astype(F32)
-                rl_tx[layer, s, way, k] = both.astype(BF16)
-                remote(
-                    rl_tx.at[layer, s, way, k],
-                    rs_rx.at[layer, s, 1 + way, core, halves[way]],
-                    send,
-                    recv.at[1 + way],
-                    2 * chip + k,
-                )
-        leaving.append(lambda: arrived(ag_rx.at[layer, s, pl.ds(0, 2)], send))
+        leaving.append(lambda: arrived(ag_rx.at[layer, s, pl.ds(0, 7)], send))
 
     def add(layer, s):
         owed(("rs", layer, s))
         at = slice(s * WIDE, (s + 1) * WIDE)
         for hl in range(2):
             total = rs_rx[layer, s, 0, hl].astype(F32)
-            for slot in range(1, 3):
+            for slot in range(1, 4):
                 total = total + rs_rx[layer, s, slot, hl].astype(F32)
             out[hl, :, at] = out[hl, :, at] + total.astype(BF16).astype(F32)
         if layer + 1 < LAYERS:
@@ -479,27 +519,28 @@
         for s in range(NS):
             then(name, f, layer, s)
 
-    then("wy", wy, 0)
     each("stats", send_stats, 0)
     then("near", hear_near)
-    then("wz", wz, 0, 1)
+    then("wd", wd)
     then("small", send_small)
     then("wy", wy, 1)
     then("far", hear_far)
     each("there", there, 0)
-    then("wz", wz, 0, 2)
     then("filters", filters)
     then("columns", columns)
-    each("transform", transform, 0)
-    then("wz", wz, 0, 3)
+    then("wr", wr, 0)
+    then("transform", transform, 0, 0)
+    then("wr", wr, 1)
+    then("transform", transform, 0, 1)
+    then("ws", ws, 0)
+    then("ws", ws, 1)
+    then("we", we, 0)
     each("share", share, 0)
-    then("wz", wz, 0, 4)
-    then("wc", wc, 0)
+    then("we", we, 1)
     then("wz", wz, 1, 1)
     then("weights", weights, 0)
     then("wz", wz, 1, 2)
     each("mlp", mlp, 0)
-    each("relay", relay, 0)
     then("wz", wz, 1, 3)
     each("add", add, 0)
     each("there", there, 1)
@@ -509,7 +550,6 @@
     each("share", share, 1)
     then("weights", weights, 1)
     each("mlp", mlp, 1)
-    each("relay", relay, 1)
     each("add", add, 1)
 
     for _, step in plan[:STOP]:
@@ -541,9 +581,7 @@
         pltpu.VMEM((LAYERS, NS, 2, CH, WIDE), BF16),
         pltpu.VMEM((LAYERS, NS, NC, CH, WIDE), BF16),
         pltpu.VMEM((LAYERS, NS, NC, CH, WIDE), BF16),
-        pltpu.VMEM((LAYERS, NS, 3, 2, CH, WIDE), BF16),
-        pltpu.VMEM((LAYERS, NS, 2, 2, CH // 2, WIDE), BF16),
-        pltpu.VMEM((LAYERS, NS, 2, 2, CH // 2, WIDE), BF16),
+        pltpu.VMEM((LAYERS, NS, 4, 2, CH, WIDE), BF16),
         pltpu.VMEM((LAYERS, 2, NZ, NY, 6, 8, HID), BF16),
         pltpu.VMEM((LAYERS, 768, 768), BF16),
         pltpu.VMEM((LAYERS, 768, 768), BF16),
@@ -557,9 +595,9 @@
     ]
     scratch += [dma((LAYERS, NS))] * 6
     scratch += [dma((LAYERS, NS)), dma((LAYERS, NS, 4))]
-    scratch += [dma((LAYERS, NS, 2)), dma((LAYERS, NS, 5))]
+    scratch += [dma((LAYERS, NS)), dma((LAYERS, NS, 4))]
     scratch += [dma((LAYERS, NY))] * 2 + [dma((LAYERS, 4, 2))] * 2 + [dma((LAYERS,))] * 2
-    scratch += [pltpu.SemaphoreType.REGULAR] * 2
+    scratch += [pltpu.SemaphoreType.REGULAR] * 2 + [dma((NZ,))]
     return pl.pallas_call(
         kernel,
         out_shape=pltpu.VMEM(tokens.shape, F32),

time: 89.2 us -> 85.9 us (0.963)
  Pallas kernels: 88.3 us -> 85 us
    pallas_call x1, Pallas kernels: 88.3 us -> 85 us  [per_device(): pl.pallas_call(kernel, out_shape=pltpu.VMEM(tokens.shape, F32), in_specs=...]
where the time goes in v6:
time: 85.9 us; the launch traced here: 85.8 us
  Pallas kernels  85 us (99%)
    pallas_call x1, Pallas kernels, per_device(): pl.pallas_call(kernel, out_shape=pltpu.VMEM(tokens.shape, F32), in_specs=...  85 us

profile of v6, /device:TPU:1, one launch (start us, length us, event | category | flops | bytes accessed | tf_op | source)
XLA Modules:
  0.0 85.8 jit_solution(8650925533705664075)
XLA Ops:
  0.0 85.0 %blocks.1 = f32[2,96,512]{2,1,0:T(8,128)S(1)} custom-call(f32[2,96,512]{2,1,0:T(8,128)} %refs_0_.1, f32[2,64,96,128]{3,2,1,0:T(8,128)} %refs_1_.1, f32[2,96]{1,0:T(2,128)} %refs_2_.1, f32[2,96]{1,0:T(2,128)} %refs_3_.1, bf16[2,3,8,384]{3,2,1,0:T(8,128)(2,1)} %bitcast.4, bf16[2,384]{1,0:T(2,128)(2,1)} %refs_5_.1, bf16[2,3,8,384]{3,2,1,0:T(8,128)(2,1)} %bitcast.5, ...), custom_call_target="tpu_custom_call" | custom-call | tf_op jit(solution)/shard_map/blocks/pallas_call | solution.py:601
  85.0 0.7 copy.15

commit v7 on v6

--- a/solution.py
+++ b/solution.py
@@ -159,7 +159,8 @@
         leaving.append(lambda: arrived(target.at[pl.ds(0, NC - 1)], send))
 
     def send_stats(layer, s):
-        put_stats(layer, s)
+        if layer:
+            put_stats(layer, s)
         buf = stats_rx.at[layer, s]
         to_all(("stats", layer, s), buf, stats_s.at[layer, s], stats_r.at[layer, s])
 
@@ -174,7 +175,10 @@
                 pending["spec", layer, i] = spec_copy(layer, i).wait
         small_rx[c] = jnp.zeros((4, PIX), F32)
         turn[...] = jnp.zeros((128, 128), F32)
-        for copy in loads:
+        loads[0].wait()
+        for s in range(NS):
+            put_stats(0, s)
+        for copy in loads[1:]:
             copy.wait()
         small_rx[c, 0:2, 0:CH] = gm_buf[...]
         small_rx[c, 2:4, 0:HID] = b_buf[...].astype(F32)
@@ -299,20 +303,29 @@
     def shards(count):
         return w_all.at[0, core, pl.ds(0, count), 0]
 
+    def along_z(ref, t, dz):
+        pltpu.make_async_remote_copy(
+            src_ref=ref,
+            dst_ref=ref,
+            send_sem=wy_s.at[0, 0],
+            recv_sem=wd_r.at[dz],
+            device_id=((z + t) % NZ * NY + y, c),
+            device_id_type=MESH,
+        ).start()
+        pending["wd", dz] = lambda: arrived(shard(dz, 0), wd_r.at[dz])
+
     def wd():
-        own = shard(0, 0)
-        for t in (1, 7, 2, 6, 3, 5, 4):
-            pltpu.make_async_remote_copy(
-                src_ref=own,
-                dst_ref=own,
-                send_sem=wy_s.at[0, 0],
-                recv_sem=wd_r.at[NZ - t],
-                device_id=((z + t) % NZ * NY + y, c),
-                device_id_type=MESH,
-            ).start()
-            pending["wd", t] = lambda t=t: arrived(shard(t, 0), wd_r.at[t])
+        for t in (2, 6, 1, 7):
+            along_z(shard(0, 0), t, NZ - t)
         leaving.append(lambda: arrived(shards(NZ - 1), wy_s.at[0, 0]))
         leaving.append(lambda: arrived(w_all.at[0, core, pl.ds(0, 6)], wz_s.at[0, 0, 0]))
+
+    def wf():
+        owed(("wd", 2))
+        owed(("wd", 6))
+        along_z(shard(6, 0), 2, 4)
+        along_z(shard(6, 0), 1, 5)
+        along_z(shard(2, 0), 7, 3)
 
     def round_y(ref, way, sem):
         to = (y + 1) % NY if way == 0 else (y + NY - 1) % NY
@@ -328,7 +341,7 @@
     def wr(group):
         members = (near_z, far_z)[group]
         for dz in members:
-            if dz:
+            if ("wd", dz) in pending:
                 owed(("wd", dz))
         for way in range(2):
             sem = wz_r.at[0, group, way]
@@ -526,9 +539,10 @@
     then("wy", wy, 1)
     then("far", hear_far)
     each("there", there, 0)
+    then("wf", wf)
+    then("wr", wr, 0)
     then("filters", filters)
     then("columns", columns)
-    then("wr", wr, 0)
     then("transform", transform, 0, 0)
     then("wr", wr, 1)
     then("transform", transform, 0, 1)

time: 85.9 us -> 85.7 us (level)
  no operation moved by 1% of the time
where the time goes in v7:
time: 85.7 us; the launch traced here: 85.6 us
  Pallas kernels  84.8 us (99%)
    pallas_call x1, Pallas kernels, per_device(): pl.pallas_call(kernel, out_shape=pltpu.VMEM(tokens.shape, F32), in_specs=...  84.8 us

profile of v7, /device:TPU:1, one launch (start us, length us, event | category | flops | bytes accessed | tf_op | source)
XLA Modules:
  0.0 85.6 jit_solution(13542783614236215919)
XLA Ops:
  0.0 84.8 %blocks.1 = f32[2,96,512]{2,1,0:T(8,128)S(1)} custom-call(f32[2,96,512]{2,1,0:T(8,128)} %refs_0_.1, f32[2,64,96,128]{3,2,1,0:T(8,128)} %refs_1_.1, f32[2,96]{1,0:T(2,128)} %refs_2_.1, f32[2,96]{1,0:T(2,128)} %refs_3_.1, bf16[2,3,8,384]{3,2,1,0:T(8,128)(2,1)} %bitcast.4, bf16[2,384]{1,0:T(2,128)(2,1)} %refs_5_.1, bf16[2,3,8,384]{3,2,1,0:T(8,128)(2,1)} %bitcast.5, ...), custom_call_target="tpu_custom_call" | custom-call | tf_op jit(solution)/shard_map/blocks/pallas_call | solution.py:615
  84.8 0.7 copy.15
